TPU v7x, 32 devices: a 4x2x2 block of a 4x4x8 slice. The times are simulated.
32 devices in a mesh: dp: 4 (over y, z), ep: 8 (over x, core).
Axes of the slice: x: 4, y: 2, z: 2, core: 2. Of those that a mesh axis runs over, the one named last changes fastest.
The devices are a block of a 4x4x8 slice.
Arguments:
- dy_home: bfloat16 [4096, 1024], P(('dp', 'ep')), parts along dimension 0
- topk_idx: int32 [4096, 8], P(('dp', 'ep')), parts along dimension 0
- slot_idx: int32 [4096, 8], P(('dp', 'ep')), parts along dimension 0
- gates: float32 [4096, 8], P(('dp', 'ep')), parts along dimension 0
- y_back: bfloat16 [4096, 8, 1024], P(('dp', 'ep')), parts along dimension 0
- x_disp: bfloat16 [128, 512, 1024], P(('dp', 'ep')), parts along dimension 0
- h1_disp: bfloat16 [128, 512, 512], P(('dp', 'ep')), parts along dimension 0
- h3_disp: bfloat16 [128, 512, 512], P(('dp', 'ep')), parts along dimension 0
- w_gate: bfloat16 [32, 1024, 512], P('ep')
- w_up: bfloat16 [32, 1024, 512], P('ep')
- w_down: bfloat16 [32, 512, 1024], P('ep')
Outputs:
- output 1: bfloat16 [4096, 1024], P(('dp', 'ep')), parts along dimension 0
- output 2: float32 [4096, 8], P(('dp', 'ep')), parts along dimension 0
- output 3: float32 [128, 1024, 512], P(('dp', 'ep')), parts along dimension 0
- output 4: float32 [128, 1024, 512], P(('dp', 'ep')), parts along dimension 0
- output 5: float32 [128, 512, 1024], P(('dp', 'ep')), parts along dimension 0
There are 4 independent parts. A program takes and returns all parts, laid end to end along the dimension named above; an argument that names none is the same for every part.
All inputs are finite; a program needn't handle non-finite values.
Results may differ from a plain program's by a relative error of at most 0.0149677.
Values are sent between devices in bfloat16 or wider.
A program may use at most 768 MiB of HBM per device.

v0:
```python
import jax
import jax.numpy as jnp
from jax import lax
from jax.sharding import PartitionSpec as P


def gated_buffer(dy_rows, gates, flat_pos, rows_all):
    num_choice = flat_pos.size
    choice_of = jnp.full((rows_all,), num_choice, jnp.int32).at[flat_pos.reshape(-1)].set(
        jnp.arange(num_choice, dtype=jnp.int32), mode='drop')
    gate_pad = jnp.concatenate([gates.reshape(-1), jnp.zeros((1,), jnp.float32)])
    row_gate = gate_pad[choice_of]
    row_tok = jnp.minimum(choice_of // gates.shape[1], dy_rows.shape[0] - 1)
    row_dy = jnp.take(dy_rows, row_tok, axis=0)
    return (row_gate[:, None] * row_dy.astype(jnp.float32)).astype(jnp.bfloat16)


def expert_backward(dy_disp, x_disp, h_gate, h_up, w_gate, w_up, w_down):
    gate_f = h_gate.astype(jnp.float32)
    up_f = h_up.astype(jnp.float32)
    sig_gate = jax.nn.sigmoid(gate_f)
    silu_g = gate_f * sig_gate
    hidden_act = (silu_g * up_f).astype(jnp.bfloat16)
    d_act = jnp.einsum('erd,efd->erf', dy_disp, w_down, preferred_element_type=jnp.float32).astype(jnp.bfloat16).astype(jnp.float32)
    dh_gate = (d_act * up_f * sig_gate * (1.0 + gate_f * (1.0 - sig_gate))).astype(jnp.bfloat16)
    dh_up = (d_act * silu_g).astype(jnp.bfloat16)
    dw_down = jnp.einsum('erf,erd->efd', hidden_act, dy_disp, preferred_element_type=jnp.float32)
    dw_gate = jnp.einsum('erd,erf->edf', x_disp, dh_gate, preferred_element_type=jnp.float32)
    dw_up = jnp.einsum('erd,erf->edf', x_disp, dh_up, preferred_element_type=jnp.float32)
    dx_disp = (jnp.einsum('erf,edf->erd', dh_gate, w_gate, preferred_element_type=jnp.float32)
               + jnp.einsum('erf,edf->erd', dh_up, w_up, preferred_element_type=jnp.float32)).astype(jnp.bfloat16)
    return dx_disp, dw_gate, dw_up, dw_down


def solution(mesh):
    ep_size = mesh.shape['ep']
    tok_spec = P(('dp', 'ep'), None)
    buf_spec = P(('dp', 'ep'), None, None)
    expert_spec = P('ep', None, None)

    def device_step(dy_loc, topk_idx, slot_idx, gates, y_back, x_disp, h1_disp, h3_disp, w_gate, w_up, w_down):
        num_experts = w_gate.shape[0] * ep_size
        capacity = x_disp.shape[1] // ep_size
        d_model = dy_loc.shape[1]
        rows_all = num_experts * capacity
        d_gates = jnp.einsum('td,tjd->tj', dy_loc, y_back, preferred_element_type=jnp.float32)
        flat_pos = jnp.where(slot_idx >= 0, topk_idx * capacity + slot_idx, rows_all)
        send_buf = gated_buffer(dy_loc, gates, flat_pos, rows_all).reshape(num_experts, capacity, d_model)
        dy_disp = lax.all_to_all(send_buf, 'ep', 0, 1, tiled=True)
        dx_disp, dw_gate, dw_up, dw_down = expert_backward(dy_disp, x_disp, h1_disp, h3_disp, w_gate, w_up, w_down)
        dx_buf = lax.all_to_all(dx_disp, 'ep', 1, 0, tiled=True).reshape(rows_all, d_model)
        returned = jnp.take(dx_buf, flat_pos, axis=0, mode='fill', fill_value=0)
        dx_loc = jnp.sum(returned, axis=1, dtype=jnp.float32).astype(jnp.bfloat16)
        return dx_loc, d_gates, dw_gate, dw_up, dw_down

    return jax.shard_map(
        device_step, mesh=mesh,
        in_specs=(tok_spec, tok_spec, tok_spec, tok_spec, buf_spec, buf_spec, buf_spec, buf_spec,
                  expert_spec, expert_spec, expert_spec),
        out_specs=(tok_spec, tok_spec, buf_spec, buf_spec, buf_spec),
        check_vma=False)
```

profile of v0, /device:TPU:81, one launch (start us, length us, event | category | flops | bytes accessed | tf_op | source)
XLA Modules:
  0.0 187.7 jit_solution(8522863847149528381)
XLA Ops:
  0.6 0.0 copy-start
  0.6 0.9 compare_and_fusion.1
  1.5 0.1 copy.36
  1.6 0.1 reshape.72
  1.7 4.3 %scatter_custom_fusion = s32[2048]{0:T(1024)S(1)} fusion(s32[1024]{0:T(1024)S(1)} %bitcast.34, s32[1024]{0:T(1024)S(1)} %iota.3, s32[]{:T(128)} %constant.34.clone.1), kind=kCustom, calls=%fused_computation.45 | custom fusion | bytes 8196 | tf_op jit(solution)/shard_map/scatter | solution.py:9
  6.1 0.8 copy.35
  6.9 0.1 reshape.71
  7.0 0.0 copy-start.2
  7.0 11.8 %gather_fusion = f32[2048]{0:T(1024)S(1)} fusion(f32[1025]{0:T(1024)S(1)} %pad_maximum_fusion, s32[2048]{0:T(1024)S(1)} %get-tuple-element.22), kind=kCustom, calls=%fused_computation | custom fusion | bytes 24576 | tf_op jit(solution)/shard_map/gather | solution.py:12
  18.8 0.1 mul.40
  18.9 0.1 broadcast_in_dim.42
  18.9 0.0 copy-done.2
  19.0 9.6 %gather_fusion.1 = bf16[2048,1024]{1,0:T(8,128)(2,1)} fusion(bf16[128,1024]{1,0:T(8,128)(2,1)S(1)} %copy-done.2, s32[2048]{0:T(1024)S(1)} %get-tuple-element.23), kind=kCustom, calls=%fused_computation.1 | custom fusion | bytes 8396800 | tf_op jit(solution)/shard_map/jit(_take)/gather | solution.py:14
  28.6 4.2 %multiply_convert_fusion = bf16[32,64,1024]{2,1,0:T(8,128)(2,1)} fusion(bf16[32,64,1024]{2,1,0:T(8,128)(2,1)} %bitcast.30, f32[32,64]{1,0:T(8,128)S(1)} %mul.40, pred[32,64]{1,0:T(8,128)(4,1)S(1)} %broadcast_in_dim.42), kind=kLoop, calls=%fused_computation.5 | loop fusion | flops 8388608 | bytes 8398848 | tf_op jit(solution)/shard_map/convert_element_type | solution.py:15
  32.7 6.5 %all-to-all-start = ((bf16[32,64,1024]{2,1,0:T(8,128)(2,1)}), bf16[32,64,1024]{2,1,0:T(8,128)(2,1)}, u32[]{:S(2)}, u32[]{:S(2)}) async-start(bf16[32,64,1024]{2,1,0:T(8,128)(2,1)} %multiply_convert_fusion), calls=%async_computation | async-start | bytes 8388608 | tf_op jit(solution)/shard_map/all_to_all | solution.py:49
  39.2 0.0 copy-done
  39.2 1.4 fusion.12
  40.6 47.3 %all-to-all-done = bf16[32,64,1024]{2,1,0:T(8,128)(2,1)} async-done(((bf16[32,64,1024]{2,1,0:T(8,128)(2,1)}), bf16[32,64,1024]{2,1,0:T(8,128)(2,1)}, u32[]{:S(2)}, u32[]{:S(2)}) %all-to-all-start) | async-done | bytes 4194336 | tf_op jit(solution)/shard_map/all_to_all | solution.py:49
  87.9 0.0 copy-start.4
  87.9 2.8 %copy.37 = bf16[4,8,64,1024]{3,2,1,0:T(8,128)(2,1)S(1)} copy(bf16[4,8,64,1024]{3,2,0,1:T(8,128)(2,1)} %bitcast.3) | data formatting | bytes 8388608 | tf_op jit(solution)/shard_map/all_to_all | solution.py:49
  90.7 0.0 copy-start.3
  90.7 2.0 %copy-done.3 = bf16[4,8,64,1024]{3,2,1,0:T(8,128)(2,1)} copy-done((bf16[4,8,64,1024]{3,2,1,0:T(8,128)(2,1)}, bf16[4,8,64,1024]{3,2,1,0:T(8,128)(2,1)S(1)}, u32[]{:S(2)}) %copy-start.3) | copy-done | bytes 4194328
  92.7 0.0 copy-done.4
  92.7 0.0 copy-start.5
  92.7 0.0 copy-start.7
  92.7 0.0 copy-start.9
  92.7 2.4 %convolution_convert_fusion = bf16[4,512,512]{2,1,0:T(8,128)(2,1)S(1)} fusion(bf16[4,512,1024]{2,1,0:T(8,128)(2,1)S(1)} %bitcast.31, bf16[4,512,1024]{2,1,0:T(8,128)(2,1)S(1)} %copy-done.4), kind=kOutput, calls=%fused_computation.26 | convolution fusion | flops 2148532224 | bytes 10485760 | tf_op jit(solution)/shard_map/erd,efd->erf/dot_general | solution.py:24
  95.1 0.0 copy-start.11
  95.1 1.3 copy-done.11
  96.4 0.0 copy-done.5
  96.4 0.0 copy-done.7
  96.4 0.0 copy-done.9
  96.4 0.0 copy-start.6
  96.4 6.5 %fusion.24 = f32[4,512,1024]{2,1,0:T(8,128)} fusion(bf16[4,1024,512]{2,1,0:T(8,128)(2,1)S(1)} %copy-done.5, bf16[4,512,512]{2,1,0:T(8,128)(2,1)S(1)} %copy-done.7, bf16[4,512,512]{2,1,0:T(8,128)(2,1)S(1)} %convolution_convert_fusion, bf16[4,512,512]{2,1,0:T(8,128)(2,1)S(1)} %copy-done.9), kind=kOutput, calls=%fused_computation.51 | convolution fusion | flops 2161115136 | bytes 18874368 | tf_op jit(solution)/shard_map/erf,edf->erd/dot_general | solution.py:30
  102.9 0.0 copy-done.6
  102.9 7.2 %add_convert_fusion = bf16[4,512,1024]{2,1,0:T(8,128)(2,1)S(1)} fusion(f32[4,512,1024]{2,1,0:T(8,128)} %fusion.24, bf16[4,1024,512]{2,1,0:T(8,128)(2,1)S(1)} %copy-done.6, bf16[4,512,512]{2,1,0:T(8,128)(2,1)} %copy-done.11, bf16[4,512,512]{2,1,0:T(8,128)(2,1)} %param.17), kind=kOutput, calls=%fused_computation.4 | convolution fusion | flops 2160066560 | bytes 20971520 | tf_op jit(solution)/shard_map/erf,edf->erd/dot_general | solution.py:31
  110.1 5.2 %copy.38 = bf16[4,512,1024]{2,0,1:T(4,128)(2,1)} copy(bf16[4,512,1024]{2,1,0:T(8,128)(2,1)S(1)} %add_convert_fusion) | data formatting | bytes 8388608 | tf_op jit(solution)/shard_map/convert_element_type | solution.py:31
  115.3 5.7 %all-to-all-start.1 = ((bf16[4,512,1024]{2,0,1:T(4,128)(2,1)}), bf16[4,512,1024]{2,0,1:T(4,128)(2,1)}, u32[]{:S(2)}, u32[]{:S(2)}) async-start(bf16[4,512,1024]{2,0,1:T(4,128)(2,1)} %copy.38), calls=%async_computation.1 | async-start | bytes 8388608 | tf_op jit(solution)/shard_map/all_to_all | solution.py:51
  121.1 0.1 copy.40
  121.2 0.1 reshape.92
  121.3 0.1 copy.34
  121.4 0.7 copy.47
  122.1 10.5 %convolution_bitcast_fusion.1 = f32[4,1024,512]{1,2,0:T(8,128)} fusion(bf16[4,512,1024]{2,1,0:T(8,128)(2,1)} %param.16, bf16[4,512,512]{2,1,0:T(8,128)(2,1)} %param.18, bf16[4,512,512]{2,1,0:T(8,128)(2,1)} %copy-done.11, bf16[4,512,512]{2,1,0:T(8,128)(2,1)} %param.17), kind=kOutput, calls=%fused_computation.22 | convolution fusion | flops 2161115136 | bytes 18874368 | tf_op jit(solution)/shard_map/erd,erf->edf/dot_general | solution.py:28
  132.6 0.0 copy-start.10
  132.6 8.8 %copy.44 = f32[4,1024,512]{2,1,0:T(8,128)} copy(f32[4,1024,512]{1,2,0:T(8,128)} %convolution_bitcast_fusion.1) | data formatting | bytes 16777216
  141.4 0.0 copy-done.10
  141.4 8.8 %convolution_bitcast_fusion = f32[4,1024,512]{1,2,0:T(8,128)} fusion(bf16[4,512,1024]{2,1,0:T(8,128)(2,1)} %param.16, bf16[4,512,512]{2,1,0:T(8,128)(2,1)} %copy-done.11, bf16[4,512,512]{2,1,0:T(8,128)(2,1)S(1)} %copy-done.10), kind=kOutput, calls=%fused_computation.21 | convolution fusion | flops 2155872256 | bytes 16777216 | tf_op jit(solution)/shard_map/erd,erf->edf/dot_general | solution.py:29
  150.2 0.0 copy-start.8
  150.2 8.8 %copy.45 = f32[4,1024,512]{2,1,0:T(8,128)} copy(f32[4,1024,512]{1,2,0:T(8,128)} %convolution_bitcast_fusion) | data formatting | bytes 16777216
  159.0 0.0 copy-done.8
  159.0 8.8 %fusion.9 = f32[4,512,1024]{2,1,0:T(8,128)} fusion(bf16[4,512,1024]{2,1,0:T(8,128)(2,1)} %bitcast.32, bf16[4,512,512]{2,1,0:T(8,128)(2,1)S(1)} %copy-done.8, bf16[4,512,512]{2,1,0:T(8,128)(2,1)} %param.17), kind=kOutput, calls=%fused_computation.23 | convolution fusion | flops 2155872256 | bytes 16777216 | tf_op jit(solution)/shard_map/erf,erd->efd/dot_general | solution.py:27
  167.7 2.0 %all-to-all-done.1 = bf16[4,512,1024]{2,0,1:T(4,128)(2,1)} async-done(((bf16[4,512,1024]{2,0,1:T(4,128)(2,1)}), bf16[4,512,1024]{2,0,1:T(4,128)(2,1)}, u32[]{:S(2)}, u32[]{:S(2)}) %all-to-all-start.1) | async-done | bytes 4194336 | tf_op jit(solution)/shard_map/all_to_all | solution.py:51
  169.7 5.7 %copy.39 = bf16[4,8,64,1024]{3,2,0,1:T(8,128)(2,1)} copy(bf16[4,8,64,1024]{3,0,2,1:T(4,128)(2,1)} %bitcast.5) | data formatting | bytes 8388608 | tf_op jit(solution)/shard_map/all_to_all | solution.py:51
  175.4 0.0 copy-start.1
  175.4 8.9 %gather_fusion.2 = bf16[1024,1024]{1,0:T(8,128)(2,1)} fusion(bf16[2048,1024]{1,0:T(8,128)(2,1)} %bitcast.29, s32[1024]{0:T(1024)S(1)} %broadcast_clamp_fusion.1), kind=kCustom, calls=%fused_computation.2 | custom fusion | bytes 4198400 | tf_op jit(solution)/shard_map/jit(_take)/gather | solution.py:52
  184.3 3.4 %fusion.11 = bf16[128,1024]{1,0:T(8,128)(2,1)} fusion(bf16[1024,1024]{1,0:T(8,128)(2,1)} %gather_fusion.2, pred[128,8]{1,0:T(8,128)(4,1)S(1)} %copy.34), kind=kLoop, calls=%fused_computation.25 | loop fusion | flops 1966080 | bytes 2360320 | tf_op jit(solution)/shard_map/reduce_sum | solution.py:53
  187.7 0.0 copy-done.1
  (7 shorter events, 0.1 us)
Async XLA Ops:
  0.6 38.6 %copy-start = (bf16[128,8,1024]{2,1,0:T(8,128)(2,1)S(1)}, bf16[128,8,1024]{2,1,0:T(8,128)(2,1)}, u32[]{:S(2)}) copy-start(bf16[128,8,1024]{2,1,0:T(8,128)(2,1)} %param.15) | copy-start | bytes 6291460
  7.0 12.0 %copy-start.2 = (bf16[128,1024]{1,0:T(8,128)(2,1)S(1)}, bf16[128,1024]{1,0:T(8,128)(2,1)}, u32[]{:S(2)}) copy-start(bf16[128,1024]{1,0:T(8,128)(2,1)} %param.11) | copy-start | bytes 786436
  32.7 55.1 %all-to-all-start = ((bf16[32,64,1024]{2,1,0:T(8,128)(2,1)}), bf16[32,64,1024]{2,1,0:T(8,128)(2,1)}, u32[]{:S(2)}, u32[]{:S(2)}) async-start(bf16[32,64,1024]{2,1,0:T(8,128)(2,1)} %multiply_convert_fusion), calls=%async_computation | async-start | bytes 8388608 | tf_op jit(solution)/shard_map/all_to_all | solution.py:49
  87.9 4.8 %copy-start.4 = (bf16[4,512,1024]{2,1,0:T(8,128)(2,1)S(1)}, bf16[4,512,1024]{2,1,0:T(8,128)(2,1)}, u32[]{:S(2)}) copy-start(bf16[4,512,1024]{2,1,0:T(8,128)(2,1)} %param.21) | copy-start | bytes 12582916
  90.7 2.0 %copy-start.3 = (bf16[4,8,64,1024]{3,2,1,0:T(8,128)(2,1)}, bf16[4,8,64,1024]{3,2,1,0:T(8,128)(2,1)S(1)}, u32[]{:S(2)}) copy-start(bf16[4,8,64,1024]{3,2,1,0:T(8,128)(2,1)S(1)} %copy.37) | copy-start | bytes 12582916
  92.7 3.7 %copy-start.5 = (bf16[4,1024,512]{2,1,0:T(8,128)(2,1)S(1)}, bf16[4,1024,512]{2,1,0:T(8,128)(2,1)}, u32[]{:S(2)}) copy-start(bf16[4,1024,512]{2,1,0:T(8,128)(2,1)} %param.19) | copy-start | bytes 12582916
  92.7 3.7 %copy-start.7 = (bf16[4,512,512]{2,1,0:T(8,128)(2,1)S(1)}, bf16[4,512,512]{2,1,0:T(8,128)(2,1)}, u32[]{:S(2)}) copy-start(bf16[4,512,512]{2,1,0:T(8,128)(2,1)} %param.18) | copy-start | bytes 6291460
  92.7 3.7 %copy-start.9 = (bf16[4,512,512]{2,1,0:T(8,128)(2,1)S(1)}, bf16[4,512,512]{2,1,0:T(8,128)(2,1)}, u32[]{:S(2)}) copy-start(bf16[4,512,512]{2,1,0:T(8,128)(2,1)} %param.17) | copy-start | bytes 6291460
  95.1 1.3 copy-start.11
  96.4 6.5 %copy-start.6 = (bf16[4,1024,512]{2,1,0:T(8,128)(2,1)S(1)}, bf16[4,1024,512]{2,1,0:T(8,128)(2,1)}, u32[]{:S(2)}) copy-start(bf16[4,1024,512]{2,1,0:T(8,128)(2,1)} %param.20) | copy-start | bytes 12582916
  115.3 54.4 %all-to-all-start.1 = ((bf16[4,512,1024]{2,0,1:T(4,128)(2,1)}), bf16[4,512,1024]{2,0,1:T(4,128)(2,1)}, u32[]{:S(2)}, u32[]{:S(2)}) async-start(bf16[4,512,1024]{2,0,1:T(4,128)(2,1)} %copy.38), calls=%async_computation.1 | async-start | bytes 8388608 | tf_op jit(solution)/shard_map/all_to_all | solution.py:51
  132.6 8.8 %copy-start.10 = (bf16[4,512,512]{2,1,0:T(8,128)(2,1)S(1)}, bf16[4,512,512]{2,1,0:T(8,128)(2,1)}, u32[]{:S(2)}) copy-start(bf16[4,512,512]{2,1,0:T(8,128)(2,1)} %param.17) | copy-start | bytes 6291460
  150.2 8.8 %copy-start.8 = (bf16[4,512,512]{2,1,0:T(8,128)(2,1)S(1)}, bf16[4,512,512]{2,1,0:T(8,128)(2,1)}, u32[]{:S(2)}) copy-start(bf16[4,512,512]{2,1,0:T(8,128)(2,1)} %param.18) | copy-start | bytes 6291460
  175.4 12.3 %copy-start.1 = (bf16[128,8,1024]{2,1,0:T(8,128)(2,1)S(1)}, bf16[128,8,1024]{2,1,0:T(8,128)(2,1)}, u32[]{:S(2)}) copy-start(bf16[128,8,1024]{2,1,0:T(8,128)(2,1)} %param.15) | copy-start | bytes 6291460
where the time goes:
time: 188 us
  local copies, waits for them, and re-layouts  71.5 us (38%)
  waiting for transfers between devices  49.3 us (26%)
  matrix products  45.5 us (24%)
  starting transfers between devices  12.2 us (6%)
  other arithmetic  8.5 us (5%)
    all_to_all x1, waiting for transfers between devices, device_step(): dy_disp = lax.all_to_all(send_buf, 'ep', 0, 1, tiled=True)  47.3 us
    unnamed x27, local copies, waits for them, and re-layouts  21.8 us
    gather x1, local copies, waits for them, and re-layouts, gated_buffer(): row_gate = gate_pad[choice_of]  11.8 us
    dot_general x1, matrix products, expert_backward(): jnp.einsum('erd,erf->edf', x_disp, dh_gate, preferred_element_type=jnp.fl...  10.5 us
    gather x1, local copies, waits for them, and re-layouts, gated_buffer(): row_dy = jnp.take(dy_rows, row_tok, axis=0)  9.61 us
    gather x1, local copies, waits for them, and re-layouts, device_step(): returned = jnp.take(dx_buf, flat_pos, axis=0, mode='fill', fill_value=0)  8.91 us
    dot_general x1, matrix products, expert_backward(): jnp.einsum('erd,erf->edf', x_disp, dh_up, preferred_element_type=jnp.floa...  8.76 us
    dot_general x1, matrix products, expert_backward(): jnp.einsum('erf,erd->efd', hidden_act, dy_disp, preferred_element_type=jn...  8.76 us
  transfers between devices with their start and end apart: 2, of which 2 were waited for; matrix products, arithmetic and copies ran while one was open for 26% of the time, Pallas kernels for 0%

commit v1 on v0

v1 whole, which is shorter than its diff:
```python
import functools
import jax
import jax.numpy as jnp
from jax import lax
from jax.experimental import pallas as pl
from jax.experimental.pallas import tpu as pltpu
from jax.sharding import PartitionSpec as P

MESH = pl.DeviceIdType.MESH
F32 = jnp.float32
BF16 = jnp.bfloat16


def dot_nt(a, b):
    return lax.dot_general(a, b, (((1,), (1,)), ((), ())), preferred_element_type=F32)


def dot_tn(a, b):
    return lax.dot_general(a, b, (((0,), (0,)), ((), ())), preferred_element_type=F32)


def exchange_kernel(ep, cap, dy_hbm, topk_ref, slot_ref, gate_ref, yb_hbm, h1_hbm, h3_hbm, wg_hbm, wu_hbm, wd_hbm,
                    dx_ref, dg_ref, dyd_hbm, act_hbm, dh1_hbm, dh3_hbm,
                    dyall, meta, square, yb_v, h1_v, h3_v, wg_v, wu_v, wd_v, dyd_v, act_v, dh1_v, dh3_v,
                    onehot, dxd, mine, theirs, got, relay, final,
                    load_sem, meta_send, meta_recv, dy_send, dy_recv, d2d_send, d2d_recv, part_send, part_recv,
                    ring_send, ring_recv, out_sem):
    chips = ep // 2
    tok, width = dyall.shape[1], dyall.shape[2]
    half = tok // 2
    n_exp = wd_v.shape[0]
    top = topk_ref.shape[1]
    me = lax.axis_index('ep')
    chip, core = me // 2, me % 2
    right = (chip + 1) % chips
    left = (chip + chips - 1) % chips
    far = (chip + 2) % chips
    dev_r, dev_l, dev_p = right * 2 + core, left * 2 + core, chip * 2 + (1 - core)
    home_f = far * 2 + core

    def remote(src, dst, send_sem, recv_sem, dev):
        return pltpu.make_async_remote_copy(src_ref=src, dst_ref=dst, send_sem=send_sem, recv_sem=recv_sem,
                                            device_id={'ep': dev}, device_id_type=MESH)

    loads = [pltpu.make_async_copy(src, dst, load_sem.at[i]) for i, (src, dst) in enumerate((
        (dy_hbm, dyall.at[me]), (wd_hbm, wd_v), (h1_hbm, h1_v), (h3_hbm, h3_v), (wg_hbm, wg_v), (wu_hbm, wu_v),
        (yb_hbm, yb_v)))]
    for copy in loads:
        copy.start()

    slot = slot_ref[...]
    pos = jnp.where(slot >= 0, topk_ref[...] * cap + slot, -1).astype(F32)
    square[...] = jnp.zeros_like(square)
    square[:, 0:top] = pos
    square[:, top:2 * top] = gate_ref[...]
    meta[me] = square[...].T[0:2 * top, :]

    barrier = pltpu.get_barrier_semaphore()
    for d in range(1, ep):
        pl.semaphore_signal(barrier, inc=1, device_id={'ep': (me + d) % ep}, device_id_type=MESH)
    pl.semaphore_wait(barrier, ep - 1)

    metas = [remote(meta.at[me], meta.at[me], meta_send.at[d - 1], meta_recv.at[d - 1], (me + d) % ep)
             for d in range(1, ep)]
    for copy in metas:
        copy.start()
    loads[0].wait()

    def rows(home, h):
        return dyall.at[home, pl.ds(h * half, half), :]

    own_p = remote(dyall.at[me], dyall.at[me], d2d_send.at[0], d2d_recv.at[0], dev_p)
    own_p.start()
    r_0 = remote(rows(me, 0), rows(me, 0), dy_send.at[0], dy_recv.at[0], dev_r)
    l_1 = remote(rows(me, 1), rows(me, 1), dy_send.at[1], dy_recv.at[1], dev_l)
    r_1 = remote(rows(me, 1), rows(me, 1), dy_send.at[2], dy_recv.at[2], dev_r)
    l_0 = remote(rows(me, 0), rows(me, 0), dy_send.at[3], dy_recv.at[3], dev_l)
    for copy in (r_0, l_1, r_1, l_0):
        copy.start()
    f_0 = remote(rows(dev_l, 0), rows(dev_l, 0), dy_send.at[4], dy_recv.at[4], dev_r)
    f_1 = remote(rows(dev_r, 1), rows(dev_r, 1), dy_send.at[5], dy_recv.at[5], dev_l)
    left_p = remote(dyall.at[dev_l], dyall.at[dev_l], d2d_send.at[1], d2d_recv.at[1], dev_p)
    right_p = remote(dyall.at[dev_r], dyall.at[dev_r], d2d_send.at[2], d2d_recv.at[2], dev_p)
    far_p = remote(dyall.at[home_f], dyall.at[home_f], d2d_send.at[3], d2d_recv.at[3], dev_p)

    def build(home, chip_q, hc):
        table = meta[home]
        row_id = lax.broadcasted_iota(jnp.int32, (n_exp * cap, tok), 0).astype(F32) + (me * (n_exp * cap)).astype(F32)
        hit = jnp.zeros((n_exp * cap, tok), F32)
        gate = jnp.zeros((n_exp * cap, tok), F32)
        for j in range(top):
            same = row_id == table[j:j + 1, :]
            hit = jnp.where(same, 1.0, hit)
            gate = jnp.where(same, table[top + j:top + j + 1, :], gate)
        gate_row = jnp.sum(gate, axis=1, keepdims=True)
        sel = hit.astype(BF16)
        onehot[hc] = sel
        base = chip_q * (2 * cap) + hc * cap
        for n in range(width // 256):
            cols = slice(n * 256, (n + 1) * 256)
            block = (jnp.dot(sel, dyall[home, :, cols], preferred_element_type=F32) * gate_row).astype(BF16)
            for e in range(n_exp):
                dyd_v[e, pl.ds(base, cap), cols] = block[e * cap:(e + 1) * cap]

    def experts(chip_q):
        span = pl.ds(chip_q * (2 * cap), 2 * cap)

        def one(e, carry):
            d_act = dot_nt(dyd_v[e, span, :], wd_v[e]).astype(BF16).astype(F32)
            gate_f = h1_v[e, span, :].astype(F32)
            up_f = h3_v[e, span, :].astype(F32)
            sig = jax.nn.sigmoid(gate_f)
            silu = gate_f * sig
            act_v[e, span, :] = (silu * up_f).astype(BF16)
            dh1 = (d_act * up_f * sig * (1.0 + gate_f * (1.0 - sig))).astype(BF16)
            dh3 = (d_act * silu).astype(BF16)
            dh1_v[e, span, :] = dh1
            dh3_v[e, span, :] = dh3
            out = (dot_nt(dh1, wg_v[e]) + dot_nt(dh3, wu_v[e])).astype(BF16)
            at = pl.ds(pl.multiple_of(e * cap, cap), cap)
            dxd[0, at, :] = out[0:cap]
            dxd[1, at, :] = out[cap:2 * cap]
            return carry
        lax.fori_loop(0, n_exp, one, 0)

    def combine(chip_q):
        theirs[chip_q] = dot_tn(onehot[1 - core], dxd[1 - core])
        mine[chip_q] = dot_tn(onehot[core], dxd[core])

    def chunk(chip_q):
        for hc in range(2):
            build(chip_q * 2 + hc, chip_q, hc)
        experts(chip_q)
        combine(chip_q)

    parts = {}

    def send_part(name, i, chip_q):
        parts[name] = remote(theirs.at[chip_q], got.at[chip_q], part_send.at[i], part_recv.at[i], dev_p)
        parts[name].start()

    def add_part(name, chip_q):
        parts[name].wait_recv()
        mine[chip_q] = mine[chip_q] + got[chip_q]

    for copy in metas:
        copy.wait_recv()
    own_p.wait_recv()
    for copy in loads[1:6]:
        copy.wait()
    chunk(chip)
    r_0.wait_recv()
    f_0.start()
    l_1.wait_recv()
    f_1.start()
    send_part('own', 0, chip)

    loads[6].wait()

    def gate_grad(i, carry):
        at = pl.ds(pl.multiple_of(i * 16, 16), 16)
        prod = yb_v[at].astype(F32) * dyall[me, at, :].astype(F32)[:, None, :]
        dg_ref[at, :] = jnp.sum(prod, axis=-1)
        return carry
    lax.fori_loop(0, tok // 16, gate_grad, 0)

    r_1.wait_recv()
    left_p.start()
    l_0.wait_recv()
    right_p.start()
    left_p.wait_recv()
    chunk(left)
    send_part('left', 1, left)
    right_p.wait_recv()
    chunk(right)
    send_part('right', 2, right)
    f_0.wait_recv()
    f_1.wait_recv()
    far_p.start()
    add_part('left', left)
    add_part('right', right)

    def piece(ref, h):
        return ref.at[pl.ds(h * half, half), :]

    one_r = remote(piece(mine.at[right], 1), piece(final.at[0], 1), ring_send.at[0], ring_recv.at[0], dev_r)
    one_l = remote(piece(mine.at[left], 0), piece(final.at[1], 0), ring_send.at[1], ring_recv.at[1], dev_l)
    one_r.start()
    one_l.start()
    far_p.wait_recv()
    chunk(far)
    send_part('far', 3, far)
    outs = [pltpu.make_async_copy(src, dst, out_sem.at[i]) for i, (src, dst) in enumerate((
        (dyd_v, dyd_hbm), (act_v, act_hbm), (dh1_v, dh1_hbm), (dh3_v, dh3_hbm)))]
    for copy in outs:
        copy.start()
    add_part('far', far)
    two_r = remote(piece(mine.at[far], 0), relay.at[0], ring_send.at[2], ring_recv.at[2], dev_r)
    two_l = remote(piece(mine.at[far], 1), relay.at[1], ring_send.at[3], ring_recv.at[3], dev_l)
    two_r.start()
    two_l.start()
    add_part('own', chip)
    two_r.wait_recv()
    mine[right, 0:half, :] = mine[right, 0:half, :] + relay[0]
    two_l.wait_recv()
    mine[left, half:tok, :] = mine[left, half:tok, :] + relay[1]
    three_r = remote(piece(mine.at[right], 0), piece(final.at[0], 0), ring_send.at[4], ring_recv.at[4], dev_r)
    three_l = remote(piece(mine.at[left], 1), piece(final.at[1], 1), ring_send.at[5], ring_recv.at[5], dev_l)
    three_r.start()
    three_l.start()
    for copy in (one_r, one_l, three_r, three_l):
        copy.wait_recv()
    dx_ref[...] = (mine[chip] + final[0] + final[1]).astype(BF16)

    for copy in metas + [own_p, r_0, l_1, r_1, l_0, f_0, f_1, left_p, right_p, far_p] + list(parts.values()) + [
            one_r, one_l, two_r, two_l, three_r, three_l]:
        copy.wait_send()
    for copy in outs:
        copy.wait()


def exchange(ep, dy, topk, slot, gates, y_back, h1, h3, w_gate, w_up, w_down):
    tok, width = dy.shape
    n_exp, rows_e, ff = h1.shape
    cap = rows_e // ep
    chips = ep // 2
    top = topk.shape[1]
    any_spec = pl.BlockSpec(memory_space=pl.ANY)
    vmem_spec = pl.BlockSpec(memory_space=pltpu.VMEM)
    dma = pltpu.SemaphoreType.DMA
    return pl.pallas_call(
        functools.partial(exchange_kernel, ep, cap),
        out_shape=(
            jax.ShapeDtypeStruct((tok, width), BF16),
            jax.ShapeDtypeStruct((tok, top), F32),
            jax.ShapeDtypeStruct((n_exp, rows_e, width), BF16),
            jax.ShapeDtypeStruct((n_exp, rows_e, ff), BF16),
            jax.ShapeDtypeStruct((n_exp, rows_e, ff), BF16),
            jax.ShapeDtypeStruct((n_exp, rows_e, ff), BF16),
        ),
        in_specs=[any_spec, vmem_spec, vmem_spec, vmem_spec] + [any_spec] * 6,
        out_specs=(vmem_spec, vmem_spec) + (any_spec,) * 4,
        scratch_shapes=[
            pltpu.VMEM((ep, tok, width), BF16),
            pltpu.VMEM((ep, 2 * top, tok), F32),
            pltpu.VMEM((tok, tok), F32),
            pltpu.VMEM((tok, top, width), BF16),
            pltpu.VMEM((n_exp, rows_e, ff), BF16),
            pltpu.VMEM((n_exp, rows_e, ff), BF16),
            pltpu.VMEM((n_exp, width, ff), BF16),
            pltpu.VMEM((n_exp, width, ff), BF16),
            pltpu.VMEM((n_exp, ff, width), BF16),
            pltpu.VMEM((n_exp, rows_e, width), BF16),
            pltpu.VMEM((n_exp, rows_e, ff), BF16),
            pltpu.VMEM((n_exp, rows_e, ff), BF16),
            pltpu.VMEM((n_exp, rows_e, ff), BF16),
            pltpu.VMEM((2, n_exp * cap, tok), BF16),
            pltpu.VMEM((2, n_exp * cap, width), BF16),
            pltpu.VMEM((chips, tok, width), F32),
            pltpu.VMEM((chips, tok, width), F32),
            pltpu.VMEM((chips, tok, width), F32),
            pltpu.VMEM((2, tok // 2, width), F32),
            pltpu.VMEM((2, tok, width), F32),
            dma((7,)), dma((ep - 1,)), dma((ep - 1,)), dma((6,)), dma((6,)), dma((4,)), dma((4,)),
            dma((4,)), dma((4,)), dma((6,)), dma((6,)), dma((4,)),
        ],
        compiler_params=pltpu.CompilerParams(collective_id=0, has_side_effects=True, vmem_limit_bytes=60 * 2**20),
        name='exchange',
    )(dy, topk, slot, gates, y_back, h1, h3, w_gate, w_up, w_down)


def weight_grad_kernel(x_ref, dyd_ref, act_ref, dh1_ref, dh3_ref, dwg_ref, dwu_ref, dwd_ref):
    dwd_ref[0] = dot_tn(act_ref[0], dyd_ref[0])
    dwg_ref[0] = dot_tn(x_ref[0], dh1_ref[0])
    dwu_ref[0] = dot_tn(x_ref[0], dh3_ref[0])


def weight_grads(x, dyd, act, dh1, dh3):
    n_exp, rows_e, width = x.shape
    ff = act.shape[2]
    wide = pl.BlockSpec((1, rows_e, width), lambda e: (e, 0, 0))
    thin = pl.BlockSpec((1, rows_e, ff), lambda e: (e, 0, 0))
    tall = pl.BlockSpec((1, width, ff), lambda e: (e, 0, 0))
    flat = pl.BlockSpec((1, ff, width), lambda e: (e, 0, 0))
    return pl.pallas_call(
        weight_grad_kernel,
        grid=(n_exp,),
        out_shape=(
            jax.ShapeDtypeStruct((n_exp, width, ff), F32),
            jax.ShapeDtypeStruct((n_exp, width, ff), F32),
            jax.ShapeDtypeStruct((n_exp, ff, width), F32),
        ),
        in_specs=[wide, wide, thin, thin, thin],
        out_specs=(tall, tall, flat),
        compiler_params=pltpu.CompilerParams(vmem_limit_bytes=48 * 2**20),
        name='weight_grads',
    )(x, dyd, act, dh1, dh3)


def solution(mesh):
    ep = mesh.shape['ep']
    tok_spec = P(('dp', 'ep'), None)
    buf_spec = P(('dp', 'ep'), None, None)
    expert_spec = P('ep', None, None)

    def device_step(dy, topk_idx, slot_idx, gates, y_back, x_disp, h1_disp, h3_disp, w_gate, w_up, w_down):
        dx, d_gates, dyd, act, dh1, dh3 = exchange(
            ep, dy, topk_idx, slot_idx, gates, y_back, h1_disp, h3_disp, w_gate, w_up, w_down)
        dw_gate, dw_up, dw_down = weight_grads(x_disp, dyd, act, dh1, dh3)
        return dx, d_gates, dw_gate, dw_up, dw_down

    return jax.shard_map(
        device_step, mesh=mesh,
        in_specs=(tok_spec, tok_spec, tok_spec, tok_spec, buf_spec, buf_spec, buf_spec, buf_spec,
                  expert_spec, expert_spec, expert_spec),
        out_specs=(tok_spec, tok_spec, buf_spec, buf_spec, buf_spec),
        check_vma=False)
```

time: 188 us -> 79.5 us (0.42)
  Pallas kernels: 0 us -> 68.9 us
  local copies, waits for them, and re-layouts: 71.5 us -> 9.63 us
  waiting for transfers between devices: 49.3 us -> 0 us
  matrix products: 45.5 us -> 0 us
  starting transfers between devices: 12.2 us -> 0 us
  other arithmetic: 8.5 us -> 0 us
    pallas_call x0 -> x2, Pallas kernels: none -> 68.9 us  [the longest x1 55 us: exchange(): pl.pallas_call(functools.partial(exchange_kernel, ep, cap), out_shape=(ja...]
    all_to_all x2 -> x0, waiting for transfers between devices: 49.3 us -> none  [the longest x1 47.3 us: device_step(): dy_disp = lax.all_to_all(send_buf, 'ep', 0, 1, tiled=True)]
    dot_general x7 -> x0, matrix products: 45.5 us -> none  [the longest x1 10.5 us: expert_backward(): jnp.einsum('erd,erf->edf', x_disp, dh_gate, preferred_element_type=jnp.fl...]
    gather x3 -> x0, local copies, waits for them, and re-layouts: 30.3 us -> none  [the longest x1 11.8 us: gated_buffer(): row_gate = gate_pad[choice_of]]
    all_to_all x2 -> x0, starting transfers between devices: 12.2 us -> none  [the longest x1 6.47 us: device_step(): dy_disp = lax.all_to_all(send_buf, 'ep', 0, 1, tiled=True)]
    unnamed x27 -> x11, local copies, waits for them, and re-layouts: 21.8 us -> 9.63 us
    all_to_all x2 -> x0, local copies, waits for them, and re-layouts: 8.51 us -> none  [the longest x1 5.68 us: device_step(): lax.all_to_all(dx_disp, 'ep', 1, 0, tiled=True).reshape(rows_all, d_model)]
    convert_element_type x1 -> x0, local copies, waits for them, and re-layouts: 5.21 us -> none  [expert_backward(): dx_disp = (jnp.einsum('erf,edf->erd', dh_gate, w_gate, preferred_element_...]
  transfers between devices with their start and end apart: 2 -> 0, of which waited for: 2 -> 0; matrix products, arithmetic and copies ran while one was open for 26% -> 0% of each run, Pallas kernels for 0% -> 0%
where the time goes in v1:
time: 79.5 us; the launch traced here: 79.1 us
  Pallas kernels  68.9 us (87%)
  local copies, waits for them, and re-layouts  9.63 us (12%)
    pallas_call x1, Pallas kernels, exchange(): pl.pallas_call(functools.partial(exchange_kernel, ep, cap), out_shape=(ja...  55 us
    pallas_call x1, Pallas kernels, weight_grads(): pl.pallas_call(weight_grad_kernel, grid=(n_exp,), out_shape=(jax.ShapeDty...  13.8 us
    unnamed x11, local copies, waits for them, and re-layouts  9.63 us

profile of v1, /device:TPU:81, one launch (start us, length us, event | category | flops | bytes accessed | tf_op | source)
XLA Modules:
  0.0 79.1 jit_solution(12162465253421687099)
XLA Ops:
  0.6 1.4 %copy.16.topk_ref = s32[128,8]{1,0:T(8,128)} copy(s32[128,8]{0,1:T(8,128)} %param.12) | data formatting | bytes 8192 | tf_op args[1]
  2.0 1.4 %copy.17.slot_ref = s32[128,8]{1,0:T(8,128)} copy(s32[128,8]{0,1:T(8,128)} %param.13) | data formatting | bytes 8192 | tf_op args[2]
  3.5 1.4 %copy.18.gate_ref = f32[128,8]{1,0:T(8,128)} copy(f32[128,8]{0,1:T(8,128)} %param.14) | data formatting | bytes 8192 | tf_op args[3]
  4.9 55.0 %exchange.1 = (bf16[128,1024]{1,0:T(8,128)(2,1)}, f32[128,8]{1,0:T(8,128)}, bf16[4,512,1024]{2,1,0:T(8,128)(2,1)}, bf16[4,512,512]{2,1,0:T(8,128)(2,1)}, bf16[4,...) custom-call(bf16[128,1024]{1,0:T(8,128)(2,1)} %dy_hbm.1, s32[128,8]{1,0:T(8,128)} %copy.16.topk_ref, ...), custom_call_target="tpu_custom_call" | custom-call | tf_op jit(solution)/shard_map/exchange/pallas_call | solution.py:231
  59.9 1.5 %copy.19 = f32[128,8]{0,1:T(8,128)} copy(f32[128,8]{1,0:T(8,128)} %get-tuple-element.24) | data formatting | bytes 8192
  61.4 0.0 copy-start
  61.4 1.6 %copy-done = bf16[4,512,512]{2,1,0:T(8,128)(2,1)S(1)} copy-done((bf16[4,512,512]{2,1,0:T(8,128)(2,1)S(1)}, bf16[4,512,512]{2,1,0:T(8,128)(2,1)}, u32[]{:S(2)}) %copy-start) | copy-done | bytes 2097176
  63.0 0.0 copy-start.1
  63.0 1.6 %copy-done.1 = bf16[4,512,512]{2,1,0:T(8,128)(2,1)S(1)} copy-done((bf16[4,512,512]{2,1,0:T(8,128)(2,1)S(1)}, bf16[4,512,512]{2,1,0:T(8,128)(2,1)}, u32[]{:S(2)}) %copy-start.1) | copy-done | bytes 2097176
  64.6 0.0 copy-start.2
  64.6 13.8 %weight_grads.1 = (f32[4,1024,512]{2,1,0:T(8,128)}, f32[4,1024,512]{2,1,0:T(8,128)}, f32[4,512,1024]{2,1,0:T(8,128)}) custom-call(bf16[4,512,1024]{2,1,0:T(8,128)(2,1)} %x_ref.1, bf16[4,512,1024]{2,1,0:T(8,128)(2,1)} %get-tuple-element.16.dyd_ref, bf16[4,512,512]{2,1,0:T(8,128)(2,1)S(1)} %copy-done, bf16[4,512,512]{2,1,0:T(8,128)(2,1)S(1)} %copy-done.1, ...), custom_call_target="tpu_custom_call" | custom-call | tf_op jit(solution)/shard_map/weight_grads/pallas_call | solution.py:285
  78.4 0.0 copy-done.2
  78.4 0.7 copy.21
Async XLA Ops:
  61.4 1.6 %copy-start = (bf16[4,512,512]{2,1,0:T(8,128)(2,1)S(1)}, bf16[4,512,512]{2,1,0:T(8,128)(2,1)}, u32[]{:S(2)}) copy-start(bf16[4,512,512]{2,1,0:T(8,128)(2,1)} %get-tuple-element.17.act_ref) | copy-start | bytes 6291460
  63.0 1.6 %copy-start.1 = (bf16[4,512,512]{2,1,0:T(8,128)(2,1)S(1)}, bf16[4,512,512]{2,1,0:T(8,128)(2,1)}, u32[]{:S(2)}) copy-start(bf16[4,512,512]{2,1,0:T(8,128)(2,1)} %get-tuple-element.18.dh1_ref) | copy-start | bytes 6291460
  64.6 13.8 %copy-start.2 = (bf16[128,1024]{1,0:T(8,128)(2,1)S(1)}, bf16[128,1024]{1,0:T(8,128)(2,1)}, u32[]{:S(2)}) copy-start(bf16[128,1024]{1,0:T(8,128)(2,1)} %get-tuple-element.33) | copy-start | bytes 786436

commit v2 on v1

v2 whole, which is shorter than its diff:
```python
import functools
import jax
import jax.numpy as jnp
from jax import lax
from jax.experimental import pallas as pl
from jax.experimental.pallas import tpu as pltpu
from jax.sharding import PartitionSpec as P

MESH = pl.DeviceIdType.MESH
F32 = jnp.float32
BF16 = jnp.bfloat16


def dot_nt(a, b):
    return lax.dot_general(a, b, (((1,), (1,)), ((), ())), preferred_element_type=F32)


def dot_tn(a, b):
    return lax.dot_general(a, b, (((0,), (0,)), ((), ())), preferred_element_type=F32)


def exchange_kernel(ep, cap, dy_hbm, topk_ref, slot_ref, gate_ref, yb_hbm, x_hbm, h1_hbm, h3_hbm, wg_hbm, wu_hbm, wd_hbm,
                    dx_ref, dg_ref, x_v, dyd_v, act_v, dh1_v, dh3_v,
                    dyall, meta, square, yb_v, h1_v, h3_v, silu_v, slope_v, wg_v, wu_v, wd_v,
                    onehot, dxd, mine, theirs, got, relay, final,
                    load_sem, row_sem, meta_send, meta_recv, dy_send, dy_recv, d2d_send, d2d_recv, part_send, part_recv,
                    ring_send, ring_recv):
    chips = ep // 2
    tok, width = dyall.shape[1], dyall.shape[2]
    half = tok // 2
    n_exp = wd_v.shape[0]
    top = topk_ref.shape[0]
    pair = 2 * cap
    me = lax.axis_index('ep')
    chip, core = me // 2, me % 2
    right = (chip + 1) % chips
    left = (chip + chips - 1) % chips
    far = (chip + 2) % chips
    dev_r, dev_l, dev_p = right * 2 + core, left * 2 + core, chip * 2 + (1 - core)
    home_f = far * 2 + core
    chip_at = (chip, left, right, far)

    def remote(src, dst, send_sem, recv_sem, dev):
        return pltpu.make_async_remote_copy(src_ref=src, dst_ref=dst, send_sem=send_sem, recv_sem=recv_sem,
                                            device_id={'ep': dev}, device_id_type=MESH)

    def by_rows(src, dst, i):
        return [pltpu.make_async_copy(src.at[:, pl.ds(chip_at[p] * pair, pair), :],
                                      dst.at[:, pl.ds(p * pair, pair), :], row_sem.at[i, p]) for p in range(chips)]

    own_load = pltpu.make_async_copy(dy_hbm, dyall.at[me], load_sem.at[0])
    h_loads = by_rows(h1_hbm, h1_v, 0) + by_rows(h3_hbm, h3_v, 1)
    w_loads = [pltpu.make_async_copy(src, dst, load_sem.at[i + 1]) for i, (src, dst) in enumerate((
        (wd_hbm, wd_v), (wg_hbm, wg_v), (wu_hbm, wu_v)))]
    yb_load = pltpu.make_async_copy(yb_hbm, yb_v, load_sem.at[4])
    x_loads = by_rows(x_hbm, x_v, 2)
    for copy in [own_load] + h_loads + w_loads + [yb_load] + x_loads:
        copy.start()

    slot = slot_ref[...]
    meta[me, 0:top, :] = jnp.where(slot >= 0, topk_ref[...] * cap + slot, -1).astype(F32)
    meta[me, top:2 * top, :] = gate_ref[...]
    square[...] = jnp.zeros_like(square)

    barrier = pltpu.get_barrier_semaphore()
    for d in range(1, ep):
        pl.semaphore_signal(barrier, inc=1, device_id={'ep': (me + d) % ep}, device_id_type=MESH)
    pl.semaphore_wait(barrier, ep - 1)

    own_load.wait()

    def rows(home, h):
        return dyall.at[home, pl.ds(h * half, half), :]

    r_0 = remote(rows(me, 0), rows(me, 0), dy_send.at[0], dy_recv.at[0], dev_r)
    l_1 = remote(rows(me, 1), rows(me, 1), dy_send.at[1], dy_recv.at[1], dev_l)
    r_1 = remote(rows(me, 1), rows(me, 1), dy_send.at[2], dy_recv.at[2], dev_r)
    l_0 = remote(rows(me, 0), rows(me, 0), dy_send.at[3], dy_recv.at[3], dev_l)
    own_p = remote(dyall.at[me], dyall.at[me], d2d_send.at[0], d2d_recv.at[0], dev_p)
    metas = [remote(meta.at[me], meta.at[me], meta_send.at[d - 1], meta_recv.at[d - 1], (me + d) % ep)
             for d in range(1, ep)]
    for copy in [r_0, l_1, own_p] + metas + [r_1, l_0]:
        copy.start()
    f_0 = remote(rows(dev_l, 0), rows(dev_l, 0), dy_send.at[4], dy_recv.at[4], dev_r)
    f_1 = remote(rows(dev_r, 1), rows(dev_r, 1), dy_send.at[5], dy_recv.at[5], dev_l)
    left_p = remote(dyall.at[dev_l], dyall.at[dev_l], d2d_send.at[1], d2d_recv.at[1], dev_p)
    right_p = remote(dyall.at[dev_r], dyall.at[dev_r], d2d_send.at[2], d2d_recv.at[2], dev_p)
    far_p = remote(dyall.at[home_f], dyall.at[home_f], d2d_send.at[3], d2d_recv.at[3], dev_p)

    def factors(e, carry):
        for p in range(chips):
            span = slice(p * pair, (p + 1) * pair)
            gate_f = h1_v[e, span, :].astype(F32)
            up_f = h3_v[e, span, :].astype(F32)
            sig = jax.nn.sigmoid(gate_f)
            silu = gate_f * sig
            act_v[e, span, :] = (silu * up_f).astype(BF16)
            silu_v[e, span, :] = silu
            slope_v[e, span, :] = up_f * sig * (1.0 + gate_f * (1.0 - sig))
        return carry

    def build(p, hc):
        home = chip_at[p] * 2 + hc
        table = meta[home]
        row_id = lax.broadcasted_iota(jnp.int32, (n_exp * cap, tok), 0).astype(F32) + (me * (n_exp * cap)).astype(F32)
        hit = jnp.zeros((n_exp * cap, tok), F32)
        gate = jnp.zeros((n_exp * cap, tok), F32)
        for j in range(top):
            same = row_id == table[j:j + 1, :]
            hit = jnp.where(same, 1.0, hit)
            gate = jnp.where(same, table[top + j:top + j + 1, :], gate)
        gate_row = jnp.sum(gate, axis=1, keepdims=True)
        sel = hit.astype(BF16)
        onehot[p, hc] = sel
        base = p * pair + hc * cap
        for n in range(width // 256):
            cols = slice(n * 256, (n + 1) * 256)
            block = (jnp.dot(sel, dyall[home, :, cols], preferred_element_type=F32) * gate_row).astype(BF16)
            for e in range(n_exp):
                dyd_v[e, base:base + cap, cols] = block[e * cap:(e + 1) * cap]

    def experts(p, count):
        span = slice(p * pair, (p + count) * pair)
        for e in range(n_exp):
            d_act = dot_nt(dyd_v[e, span, :], wd_v[e]).astype(BF16).astype(F32)
            dh1 = (d_act * slope_v[e, span, :]).astype(BF16)
            dh3 = (d_act * silu_v[e, span, :]).astype(BF16)
            dh1_v[e, span, :] = dh1
            dh3_v[e, span, :] = dh3
            out = (dot_nt(dh1, wg_v[e]) + dot_nt(dh3, wu_v[e])).astype(BF16)
            for q in range(2 * count):
                dxd[p + q // 2, q % 2, e * cap:(e + 1) * cap, :] = out[q * cap:(q + 1) * cap]

    def combine(p):
        theirs[p] = dot_tn(onehot[p, 1 - core], dxd[p, 1 - core])
        mine[p] = dot_tn(onehot[p, core], dxd[p, core])

    parts = [remote(theirs.at[p], got.at[p], part_send.at[p], part_recv.at[p], dev_p) for p in range(chips)]

    def add_part(p):
        parts[p].wait_recv()
        mine[p] = mine[p] + got[p]

    for copy in h_loads:
        copy.wait()
    lax.fori_loop(0, n_exp, factors, 0)
    r_0.wait_recv()
    f_0.start()
    l_1.wait_recv()
    f_1.start()
    for copy in metas:
        copy.wait_recv()
    own_p.wait_recv()
    for hc in range(2):
        build(0, hc)
    for copy in w_loads:
        copy.wait()
    experts(0, 1)
    r_1.wait_recv()
    left_p.start()
    l_0.wait_recv()
    right_p.start()
    combine(0)
    parts[0].start()
    left_p.wait_recv()
    right_p.wait_recv()
    for p in (1, 2):
        for hc in range(2):
            build(p, hc)
    experts(1, 2)
    combine(2)
    combine(1)
    parts[2].start()
    parts[1].start()
    f_0.wait_recv()
    f_1.wait_recv()
    far_p.start()
    add_part(2)
    add_part(1)

    def piece(ref, h):
        return ref.at[pl.ds(h * half, half), :]

    one_r = remote(piece(mine.at[2], 1), piece(final.at[0], 1), ring_send.at[0], ring_recv.at[0], dev_r)
    one_l = remote(piece(mine.at[1], 0), piece(final.at[1], 0), ring_send.at[1], ring_recv.at[1], dev_l)
    one_r.start()
    one_l.start()
    far_p.wait_recv()
    for hc in range(2):
        build(3, hc)
    experts(3, 1)
    combine(3)
    parts[3].start()
    add_part(3)
    quarter = half // 2
    two, three = [], []
    for k in range(2):
        at_r, at_l, at = pl.ds(k * quarter, quarter), pl.ds(half + k * quarter, quarter), pl.ds(k * quarter, quarter)
        two.append((remote(mine.at[3, at_r, :], relay.at[0, at, :], ring_send.at[2 + k], ring_recv.at[2 + k], dev_r),
                    remote(mine.at[3, at_l, :], relay.at[1, at, :], ring_send.at[4 + k], ring_recv.at[4 + k], dev_l)))
        three.append((remote(mine.at[2, at_r, :], final.at[0, at_r, :], ring_send.at[6 + k], ring_recv.at[6 + k], dev_r),
                      remote(mine.at[1, at_l, :], final.at[1, at_l, :], ring_send.at[8 + k], ring_recv.at[8 + k], dev_l)))
    for pair_of in two:
        for copy in pair_of:
            copy.start()
    add_part(0)

    yb_load.wait()

    def gate_grad(i, carry):
        at = pl.ds(pl.multiple_of(i * 16, 16), 16)
        prod = yb_v[at].astype(F32) * dyall[me, at, :].astype(F32)[:, None, :]
        square[at, 0:top] = jnp.sum(prod, axis=-1)
        return carry
    lax.fori_loop(0, tok // 16, gate_grad, 0)
    dg_ref[...] = square[...].T[0:top, :]

    for k in range(2):
        lo, hi, at = k * quarter, half + k * quarter, slice(k * quarter, (k + 1) * quarter)
        two[k][0].wait_recv()
        mine[2, lo:lo + quarter, :] = mine[2, lo:lo + quarter, :] + relay[0, at, :]
        two[k][1].wait_recv()
        mine[1, hi:hi + quarter, :] = mine[1, hi:hi + quarter, :] + relay[1, at, :]
        three[k][0].start()
        three[k][1].start()
    one_r.wait_recv()
    one_l.wait_recv()
    for k in range(2):
        three[k][0].wait_recv()
        three[k][1].wait_recv()
    dx_ref[...] = (mine[0] + final[0] + final[1]).astype(BF16)

    for copy in metas + [own_p, r_0, l_1, r_1, l_0, f_0, f_1, left_p, right_p, far_p] + parts + [one_r, one_l] + [
            copy for group in two + three for copy in group]:
        copy.wait_send()
    for copy in x_loads:
        copy.wait()


def exchange(ep, dy, topk, slot, gates, y_back, x, h1, h3, w_gate, w_up, w_down):
    tok, width = dy.shape
    n_exp, rows_e, ff = h1.shape
    cap = rows_e // ep
    chips = ep // 2
    top = topk.shape[0]
    any_spec = pl.BlockSpec(memory_space=pl.ANY)
    vmem_spec = pl.BlockSpec(memory_space=pltpu.VMEM)
    dma = pltpu.SemaphoreType.DMA
    return pl.pallas_call(
        functools.partial(exchange_kernel, ep, cap),
        out_shape=(
            jax.ShapeDtypeStruct((tok, width), BF16),
            jax.ShapeDtypeStruct((top, tok), F32),
            pltpu.VMEM((n_exp, rows_e, width), BF16),
            pltpu.VMEM((n_exp, rows_e, width), BF16),
            pltpu.VMEM((n_exp, rows_e, ff), BF16),
            pltpu.VMEM((n_exp, rows_e, ff), BF16),
            pltpu.VMEM((n_exp, rows_e, ff), BF16),
        ),
        in_specs=[any_spec, vmem_spec, vmem_spec, vmem_spec] + [any_spec] * 7,
        out_specs=(vmem_spec,) * 7,
        scratch_shapes=[
            pltpu.VMEM((ep, tok, width), BF16),
            pltpu.VMEM((ep, 2 * top, tok), F32),
            pltpu.VMEM((tok, tok), F32),
            pltpu.VMEM((tok, top, width), BF16),
            pltpu.VMEM((n_exp, rows_e, ff), BF16),
            pltpu.VMEM((n_exp, rows_e, ff), BF16),
            pltpu.VMEM((n_exp, rows_e, ff), F32),
            pltpu.VMEM((n_exp, rows_e, ff), F32),
            pltpu.VMEM((n_exp, width, ff), BF16),
            pltpu.VMEM((n_exp, width, ff), BF16),
            pltpu.VMEM((n_exp, ff, width), BF16),
            pltpu.VMEM((chips, 2, n_exp * cap, tok), BF16),
            pltpu.VMEM((chips, 2, n_exp * cap, width), BF16),
            pltpu.VMEM((chips, tok, width), F32),
            pltpu.VMEM((chips, tok, width), F32),
            pltpu.VMEM((chips, tok, width), F32),
            pltpu.VMEM((2, tok // 2, width), F32),
            pltpu.VMEM((2, tok, width), F32),
            dma((5,)), dma((3, chips)), dma((ep - 1,)), dma((ep - 1,)), dma((6,)), dma((6,)), dma((4,)), dma((4,)),
            dma((chips,)), dma((chips,)), dma((10,)), dma((10,)),
        ],
        compiler_params=pltpu.CompilerParams(collective_id=0, has_side_effects=True, vmem_limit_bytes=46 * 2**20),
        name='exchange',
    )(dy, topk, slot, gates, y_back, x, h1, h3, w_gate, w_up, w_down)


def weight_grad_kernel(x_v, dyd_v, act_v, dh1_v, dh3_v, dwg_hbm, dwu_hbm, dwd_hbm, wide_s, thin_s, sem):
    n_exp, _, width = x_v.shape
    ff = act_v.shape[2]
    hw, hf = width // 2, ff // 2

    def one(e, carry):
        @pl.when(e > 0)
        def _():
            for u in range(6):
                slot(u, e - 1).wait()
        for u in range(2):
            wide_s[u] = dot_tn(act_v[e, :, u * hf:(u + 1) * hf], dyd_v[e])
            slot(u, e).start()
        for u in range(2):
            cols = slice(u * hw, (u + 1) * hw)
            thin_s[u] = dot_tn(x_v[e, :, cols], dh1_v[e])
            slot(2 + u, e).start()
            thin_s[2 + u] = dot_tn(x_v[e, :, cols], dh3_v[e])
            slot(4 + u, e).start()
        return carry

    def slot(u, e):
        if u < 2:
            return pltpu.make_async_copy(wide_s.at[u], dwd_hbm.at[e, pl.ds(u * hf, hf), :], sem.at[u])
        out = dwg_hbm if u < 4 else dwu_hbm
        return pltpu.make_async_copy(thin_s.at[u - 2], out.at[e, pl.ds((u % 2) * hw, hw), :], sem.at[u])

    lax.fori_loop(0, n_exp, one, 0)
    for u in range(6):
        slot(u, n_exp - 1).wait()


def weight_grads(*operands):
    n_exp, _, width = operands[0].shape
    ff = operands[2].shape[2]
    any_spec = pl.BlockSpec(memory_space=pl.ANY)
    vmem_spec = pl.BlockSpec(memory_space=pltpu.VMEM)
    return pl.pallas_call(
        weight_grad_kernel,
        out_shape=(
            jax.ShapeDtypeStruct((n_exp, width, ff), F32),
            jax.ShapeDtypeStruct((n_exp, width, ff), F32),
            jax.ShapeDtypeStruct((n_exp, ff, width), F32),
        ),
        in_specs=[vmem_spec] * 5,
        out_specs=(any_spec,) * 3,
        scratch_shapes=[pltpu.VMEM((2, ff // 2, width), F32), pltpu.VMEM((4, width // 2, ff), F32),
                        pltpu.SemaphoreType.DMA((6,))],
        compiler_params=pltpu.CompilerParams(vmem_limit_bytes=24 * 2**20),
        name='weight_grads',
    )(*[pltpu.with_memory_space_constraint(x, pltpu.VMEM) for x in operands])


def solution(mesh):
    ep = mesh.shape['ep']
    tok_spec = P(('dp', 'ep'), None)
    buf_spec = P(('dp', 'ep'), None, None)
    expert_spec = P('ep', None, None)

    def device_step(dy, topk_idx, slot_idx, gates, y_back, x_disp, h1_disp, h3_disp, w_gate, w_up, w_down):
        dx, d_gates, *saved = exchange(
            ep, dy, topk_idx.T, slot_idx.T, gates.T, y_back, x_disp, h1_disp, h3_disp, w_gate, w_up, w_down)
        dw_gate, dw_up, dw_down = weight_grads(*saved)
        return dx, d_gates.T, dw_gate, dw_up, dw_down

    return jax.shard_map(
        device_step, mesh=mesh,
        in_specs=(tok_spec, tok_spec, tok_spec, tok_spec, buf_spec, buf_spec, buf_spec, buf_spec,
                  expert_spec, expert_spec, expert_spec),
        out_specs=(tok_spec, tok_spec, buf_spec, buf_spec, buf_spec),
        check_vma=False)
```

time: 79.5 us -> 62 us (0.78)
  Pallas kernels: 68.9 us -> 59.8 us
  local copies, waits for them, and re-layouts: 9.63 us -> 1.31 us
    unnamed x11 -> x6, local copies, waits for them, and re-layouts: 9.63 us -> 1.31 us
    pallas_call x1, Pallas kernels: 55 us -> 47.3 us  [exchange(): pl.pallas_call(functools.partial(exchange_kernel, ep, cap), out_shape=(ja...]
    pallas_call x1, Pallas kernels: 13.8 us -> 12.6 us  [weight_grads(): pl.pallas_call(weight_grad_kernel, out_shape=(jax.ShapeDtypeStruct((n_exp...]
where the time goes in v2:
time: 62 us; the launch traced here: 61.8 us
  Pallas kernels  59.8 us (96%)
  local copies, waits for them, and re-layouts  1.31 us (2%)
  between operations  0.68 us (1%)
    pallas_call x1, Pallas kernels, exchange(): pl.pallas_call(functools.partial(exchange_kernel, ep, cap), out_shape=(ja...  47.3 us
    pallas_call x1, Pallas kernels, weight_grads(): pl.pallas_call(weight_grad_kernel, out_shape=(jax.ShapeDtypeStruct((n_exp...  12.6 us
    unnamed x6, local copies, waits for them, and re-layouts  1.31 us

profile of v2, /device:TPU:81, one launch (start us, length us, event | category | flops | bytes accessed | tf_op | source)
XLA Modules:
  0.0 61.8 jit_solution(14731266478926367852)
XLA Ops:
  0.6 47.3 %exchange.1 = (bf16[128,1024]{1,0:T(8,128)(2,1)}, f32[8,128]{1,0:T(8,128)}, bf16[4,512,1024]{2,1,0:T(8,128)(2,1)S(1)}, bf16[4,512,1024]{2,1,0:T(8,128)(2,1)S(1)}...) custom-call(bf16[128,1024]{1,0:T(8,128)(2,1)} %dy_hbm.1, ...), custom_call_target="tpu_custom_call" | custom-call | tf_op jit(solution)/shard_map/exchange/pallas_call | solution.py:249
  47.9 0.0 copy-start
  48.0 0.0 copy-start.1
  48.0 12.6 %weight_grads.1 = (f32[4,1024,512]{2,1,0:T(8,128)}, f32[4,1024,512]{2,1,0:T(8,128)}, f32[4,512,1024]{2,1,0:T(8,128)}) custom-call(bf16[4,512,1024]{2,1,0:T(8,128)(2,1)S(1)} %get-tuple-element.17.x_v, bf16[4,512,1024]{2,1,0:T(8,128)(2,1)S(1)} %get-tuple-element.18.dyd_v, bf16[4,512,512]{2,1,0:T(8,128)(2,1)S(1)} %get-tuple-element.19.act_v, ...), custom_call_target="tpu_custom_call" | custom-call | tf_op jit(solution)/shard_map/weight_grads/pallas_call | solution.py:326
  60.5 0.0 copy-done
  60.5 0.7 %copy.18 = bf16[128,1024]{1,0:T(8,128)(2,1)} copy(bf16[128,1024]{1,0:T(8,128)(2,1)S(1)} %copy-done) | data formatting | bytes 524288
  61.2 0.0 copy-done.1
  61.2 0.6 copy.19
Async XLA Ops:
  47.9 12.6 %copy-start = (bf16[128,1024]{1,0:T(8,128)(2,1)S(1)}, bf16[128,1024]{1,0:T(8,128)(2,1)}, u32[]{:S(2)}) copy-start(bf16[128,1024]{1,0:T(8,128)(2,1)} %get-tuple-element.30) | copy-start | bytes 786436
  48.0 13.3 %copy-start.1 = (f32[8,128]{1,0:T(8,128)S(1)}, f32[8,128]{1,0:T(8,128)}, u32[]{:S(2)}) copy-start(f32[8,128]{1,0:T(8,128)} %get-tuple-element.16) | copy-start | bytes 12292

commit v3 on v2

v3 whole, which is shorter than its diff:
```python
import functools
import jax
import jax.numpy as jnp
from jax import lax
from jax.experimental import pallas as pl
from jax.experimental.pallas import tpu as pltpu
from jax.sharding import PartitionSpec as P

MESH = pl.DeviceIdType.MESH
F32 = jnp.float32
BF16 = jnp.bfloat16


def dot_nt(a, b):
    return lax.dot_general(a, b, (((1,), (1,)), ((), ())), preferred_element_type=F32)


def dot_tn(a, b):
    return lax.dot_general(a, b, (((0,), (0,)), ((), ())), preferred_element_type=F32)


def exchange_kernel(ep, cap, dy_hbm, topk_hbm, slot_hbm, gate_hbm, yb_hbm, x_hbm, h1_hbm, h3_hbm, wg_hbm, wu_hbm, wd_hbm,
                    dx_ref, dg_ref, xt_v, dyd_v, actt_v, dh_v,
                    dyall, meta, topk_ref, slot_ref, square, yb_v, x_v, h1_v, h3_v, silu_v, slope_v, wg_v, wu_v, wd_v,
                    onehot, dxd, mine, theirs, got, relay, final,
                    load_sem, row_sem, meta_send, meta_recv, dy_send, dy_recv, d2d_send, d2d_recv, part_send, part_recv,
                    ring_send, ring_recv):
    chips = ep // 2
    tok, width = dyall.shape[1], dyall.shape[2]
    half = tok // 2
    n_exp, ff = wd_v.shape[0], wd_v.shape[1]
    top = topk_ref.shape[0]
    pair = 2 * cap
    me = lax.axis_index('ep')
    chip, core = me // 2, me % 2
    right = (chip + 1) % chips
    left = (chip + chips - 1) % chips
    far = (chip + 2) % chips
    dev_r, dev_l, dev_p = right * 2 + core, left * 2 + core, chip * 2 + (1 - core)
    home_f = far * 2 + core
    chip_at = (chip, left, right, far)
    slot_of = (1, 0, 1, 0)

    def remote(src, dst, send_sem, recv_sem, dev):
        return pltpu.make_async_remote_copy(src_ref=src, dst_ref=dst, send_sem=send_sem, recv_sem=recv_sem,
                                            device_id={'ep': dev}, device_id_type=MESH)

    def by_rows(src, dst, i):
        return [pltpu.make_async_copy(src.at[:, pl.ds(chip_at[p] * pair, pair), :],
                                      dst.at[:, pl.ds(p * pair, pair), :], row_sem.at[i, p]) for p in range(chips)]

    own_load = pltpu.make_async_copy(dy_hbm, dyall.at[me], load_sem.at[0])
    h_loads = by_rows(h1_hbm, h1_v, 0) + by_rows(h3_hbm, h3_v, 1)
    w_loads = [pltpu.make_async_copy(src, dst, load_sem.at[i + 1]) for i, (src, dst) in enumerate((
        (wd_hbm, wd_v), (wg_hbm, wg_v), (wu_hbm, wu_v)))]
    yb_load = pltpu.make_async_copy(yb_hbm, yb_v, load_sem.at[4])
    x_loads = by_rows(x_hbm, x_v, 2)
    route_loads = [pltpu.make_async_copy(topk_hbm, topk_ref, load_sem.at[5]),
                   pltpu.make_async_copy(slot_hbm, slot_ref, load_sem.at[6]),
                   pltpu.make_async_copy(gate_hbm, meta.at[me, pl.ds(top, top), :], load_sem.at[7])]

    barrier = pltpu.get_barrier_semaphore()
    for d in range(1, ep):
        pl.semaphore_signal(barrier, inc=1, device_id={'ep': (me + d) % ep}, device_id_type=MESH)
    for copy in [own_load] + route_loads + h_loads + w_loads + x_loads + [yb_load]:
        copy.start()
    square[...] = jnp.zeros_like(square)
    for copy in route_loads:
        copy.wait()
    slot = slot_ref[...]
    meta[me, 0:top, :] = jnp.where(slot >= 0, topk_ref[...] * cap + slot, -1).astype(F32)
    pl.semaphore_wait(barrier, ep - 1)

    own_load.wait()

    def rows(home, h):
        return dyall.at[home, pl.ds(h * half, half), :]

    r_0 = remote(rows(me, 0), rows(me, 0), dy_send.at[0], dy_recv.at[0], dev_r)
    l_1 = remote(rows(me, 1), rows(me, 1), dy_send.at[1], dy_recv.at[1], dev_l)
    r_1 = remote(rows(me, 1), rows(me, 1), dy_send.at[2], dy_recv.at[2], dev_r)
    l_0 = remote(rows(me, 0), rows(me, 0), dy_send.at[3], dy_recv.at[3], dev_l)
    own_p = remote(dyall.at[me], dyall.at[me], d2d_send.at[0], d2d_recv.at[0], dev_p)
    f_0 = remote(rows(dev_l, 0), rows(dev_l, 0), dy_send.at[4], dy_recv.at[4], dev_r)
    f_1 = remote(rows(dev_r, 1), rows(dev_r, 1), dy_send.at[5], dy_recv.at[5], dev_l)
    left_p = remote(dyall.at[dev_l], dyall.at[dev_l], d2d_send.at[1], d2d_recv.at[1], dev_p)
    right_p = remote(dyall.at[dev_r], dyall.at[dev_r], d2d_send.at[2], d2d_recv.at[2], dev_p)
    far_p = remote(dyall.at[home_f], dyall.at[home_f], d2d_send.at[3], d2d_recv.at[3], dev_p)
    m_r, m_l, m_p, m_f, m_lp, m_rp, m_fp = metas = [
        remote(meta.at[home], meta.at[home], meta_send.at[i], meta_recv.at[i], dev) for i, (home, dev) in enumerate((
            (me, dev_r), (me, dev_l), (me, dev_p), (dev_l, dev_r), (dev_l, dev_p), (dev_r, dev_p), (home_f, dev_p)))]
    for copy in (m_r, m_l, r_0, l_1, m_p, own_p, r_1, l_0):
        copy.start()

    def factors(e, carry):
        for p in range(chips):
            span = slice(p * pair, (p + 1) * pair)
            gate_f = h1_v[e, span, :].astype(F32)
            up_f = h3_v[e, span, :].astype(F32)
            sig = jax.nn.sigmoid(gate_f)
            silu = gate_f * sig
            actt_v[e, :, span] = (silu * up_f).astype(BF16).T
            silu_v[e, span, :] = silu
            slope_v[e, span, :] = up_f * sig * (1.0 + gate_f * (1.0 - sig))
        return carry

    def build(p, hc):
        home = chip_at[p] * 2 + hc
        table = meta[home]
        row_id = lax.broadcasted_iota(jnp.int32, (n_exp * cap, tok), 0).astype(F32) + (me * (n_exp * cap)).astype(F32)
        hit = jnp.zeros((n_exp * cap, tok), F32)
        gate = jnp.zeros((n_exp * cap, tok), F32)
        for j in range(top):
            same = row_id == table[j:j + 1, :]
            hit = jnp.where(same, 1.0, hit)
            gate = jnp.where(same, table[top + j:top + j + 1, :], gate)
        gate_row = jnp.sum(gate, axis=1, keepdims=True)
        sel = hit.astype(BF16)
        onehot[p, hc] = sel
        at = pl.ds(pl.multiple_of(p * pair + hc * cap, cap), cap)
        for n in range(width // 256):
            cols = slice(n * 256, (n + 1) * 256)
            block = (jnp.dot(sel, dyall[home, :, cols], preferred_element_type=F32) * gate_row).astype(BF16)
            for e in range(n_exp):
                dyd_v[e, at, cols] = block[e * cap:(e + 1) * cap]

    def experts(p, count):
        span = slice(p * pair, (p + count) * pair)
        for e in range(n_exp):
            d_act = dot_nt(dyd_v[e, span, :], wd_v[e]).astype(BF16).astype(F32)
            dh1 = (d_act * slope_v[e, span, :]).astype(BF16)
            dh3 = (d_act * silu_v[e, span, :]).astype(BF16)
            dh_v[e, span, 0:ff] = dh1
            dh_v[e, span, ff:2 * ff] = dh3
            out = (dot_nt(dh1, wg_v[e]) + dot_nt(dh3, wu_v[e])).astype(BF16)
            for q in range(2 * count):
                dxd[slot_of[p + q // 2], q % 2, e * cap:(e + 1) * cap, :] = out[q * cap:(q + 1) * cap]

    def sum_theirs(p):
        theirs[p] = dot_tn(onehot[p, 1 - core], dxd[slot_of[p], 1 - core])

    def sum_mine(p):
        mine[p] = dot_tn(onehot[p, core], dxd[slot_of[p], core])

    parts = [remote(theirs.at[p], got.at[p], part_send.at[p], part_recv.at[p], dev_p) for p in range(chips)]
    first, last = slice(0, half), slice(half, tok)

    def add_part(p, at):
        mine[p, at, :] = mine[p, at, :] + got[p, at, :]

    def piece(ref, h):
        return ref.at[pl.ds(h * half, half), :]

    one_r = remote(piece(mine.at[2], 1), piece(final.at[0], 1), ring_send.at[0], ring_recv.at[0], dev_r)
    one_l = remote(piece(mine.at[1], 0), piece(final.at[1], 0), ring_send.at[1], ring_recv.at[1], dev_l)
    quarter = half // 2
    two, three = [], []
    for k in range(2):
        at_r, at_l, at = pl.ds(k * quarter, quarter), pl.ds(half + k * quarter, quarter), pl.ds(k * quarter, quarter)
        two.append((remote(mine.at[3, at_r, :], relay.at[0, at, :], ring_send.at[2 + k], ring_recv.at[2 + k], dev_r),
                    remote(mine.at[3, at_l, :], relay.at[1, at, :], ring_send.at[4 + k], ring_recv.at[4 + k], dev_l)))
        three.append((remote(mine.at[2, at_r, :], final.at[0, at_r, :], ring_send.at[6 + k], ring_recv.at[6 + k], dev_r),
                      remote(mine.at[1, at_l, :], final.at[1, at_l, :], ring_send.at[8 + k], ring_recv.at[8 + k], dev_l)))

    for copy in h_loads:
        copy.wait()
    m_r.wait_recv()
    m_f.start()
    lax.fori_loop(0, n_exp, factors, 0)
    r_0.wait_recv()
    f_0.start()
    l_1.wait_recv()
    f_1.start()
    m_lp.start()
    m_l.wait_recv()
    m_rp.start()
    r_1.wait_recv()
    left_p.start()
    l_0.wait_recv()
    right_p.start()
    build(1, core)
    build(2, core)
    m_lp.wait_recv()
    left_p.wait_recv()
    build(1, 1 - core)
    m_rp.wait_recv()
    right_p.wait_recv()
    build(2, 1 - core)
    for copy in w_loads:
        copy.wait()
    experts(1, 2)
    sum_theirs(2)
    sum_theirs(1)
    sum_mine(2)
    parts[2].start()
    parts[1].start()
    sum_mine(1)
    m_f.wait_recv()
    m_fp.start()
    f_0.wait_recv()
    f_1.wait_recv()
    far_p.start()
    parts[2].wait_recv()
    add_part(2, last)
    parts[1].wait_recv()
    add_part(1, first)
    one_r.start()
    one_l.start()
    add_part(2, first)
    add_part(1, last)
    build(3, core)
    m_fp.wait_recv()
    far_p.wait_recv()
    build(3, 1 - core)
    experts(3, 1)
    sum_theirs(3)
    sum_mine(3)
    parts[3].start()
    m_p.wait_recv()
    own_p.wait_recv()
    build(0, core)
    build(0, 1 - core)
    parts[3].wait_recv()
    add_part(3, first)
    add_part(3, last)
    for group in two:
        for copy in group:
            copy.start()
    experts(0, 1)
    sum_theirs(0)
    sum_mine(0)
    parts[0].start()

    yb_load.wait()

    def gate_grad(i, carry):
        at = pl.ds(pl.multiple_of(i * 16, 16), 16)
        prod = yb_v[at].astype(F32) * dyall[me, at, :].astype(F32)[:, None, :]
        square[at, 0:top] = jnp.sum(prod, axis=-1)
        return carry
    lax.fori_loop(0, tok // 16, gate_grad, 0)
    dg_ref[...] = square[...].T[0:top, :]
    parts[0].wait_recv()
    add_part(0, first)
    add_part(0, last)

    for k in range(2):
        lo, hi, at = k * quarter, half + k * quarter, slice(k * quarter, (k + 1) * quarter)
        two[k][0].wait_recv()
        mine[2, lo:lo + quarter, :] = mine[2, lo:lo + quarter, :] + relay[0, at, :]
        two[k][1].wait_recv()
        mine[1, hi:hi + quarter, :] = mine[1, hi:hi + quarter, :] + relay[1, at, :]
        three[k][0].start()
        three[k][1].start()
    for copy in x_loads:
        copy.wait()

    def turn(e, carry):
        for p in range(chips):
            span = slice(p * pair, (p + 1) * pair)
            xt_v[e, :, span] = x_v[e, span, :].T
        return carry
    lax.fori_loop(0, n_exp, turn, 0)
    one_r.wait_recv()
    one_l.wait_recv()
    for k in range(2):
        three[k][0].wait_recv()
        three[k][1].wait_recv()
    dx_ref[...] = (mine[0] + final[0] + final[1]).astype(BF16)

    for copy in metas + [own_p, r_0, l_1, r_1, l_0, f_0, f_1, left_p, right_p, far_p] + parts + [one_r, one_l] + [
            copy for group in two + three for copy in group]:
        copy.wait_send()


def exchange(ep, dy, topk, slot, gates, y_back, x, h1, h3, w_gate, w_up, w_down):
    tok, width = dy.shape
    n_exp, rows_e, ff = h1.shape
    cap = rows_e // ep
    chips = ep // 2
    top = topk.shape[0]
    any_spec = pl.BlockSpec(memory_space=pl.ANY)
    vmem_spec = pl.BlockSpec(memory_space=pltpu.VMEM)
    dma = pltpu.SemaphoreType.DMA
    return pl.pallas_call(
        functools.partial(exchange_kernel, ep, cap),
        out_shape=(
            pltpu.VMEM((tok, width), BF16),
            pltpu.VMEM((top, tok), F32),
            pltpu.VMEM((n_exp, width, rows_e), BF16),
            pltpu.VMEM((n_exp, rows_e, width), BF16),
            pltpu.VMEM((n_exp, ff, rows_e), BF16),
            pltpu.VMEM((n_exp, rows_e, 2 * ff), BF16),
        ),
        in_specs=[any_spec] * 11,
        out_specs=(vmem_spec,) * 6,
        scratch_shapes=[
            pltpu.VMEM((ep, tok, width), BF16),
            pltpu.VMEM((ep, 2 * top, tok), F32),
            pltpu.VMEM((top, tok), jnp.int32),
            pltpu.VMEM((top, tok), jnp.int32),
            pltpu.VMEM((tok, tok), F32),
            pltpu.VMEM((tok, top, width), BF16),
            pltpu.VMEM((n_exp, rows_e, width), BF16),
            pltpu.VMEM((n_exp, rows_e, ff), BF16),
            pltpu.VMEM((n_exp, rows_e, ff), BF16),
            pltpu.VMEM((n_exp, rows_e, ff), F32),
            pltpu.VMEM((n_exp, rows_e, ff), F32),
            pltpu.VMEM((n_exp, width, ff), BF16),
            pltpu.VMEM((n_exp, width, ff), BF16),
            pltpu.VMEM((n_exp, ff, width), BF16),
            pltpu.VMEM((chips, 2, n_exp * cap, tok), BF16),
            pltpu.VMEM((2, 2, n_exp * cap, width), BF16),
            pltpu.VMEM((chips, tok, width), F32),
            pltpu.VMEM((chips, tok, width), F32),
            pltpu.VMEM((chips, tok, width), F32),
            pltpu.VMEM((2, tok // 2, width), F32),
            pltpu.VMEM((2, tok, width), F32),
            dma((8,)), dma((3, chips)), dma((7,)), dma((7,)), dma((6,)), dma((6,)), dma((4,)), dma((4,)),
            dma((chips,)), dma((chips,)), dma((10,)), dma((10,)),
        ],
        compiler_params=pltpu.CompilerParams(collective_id=0, has_side_effects=True, vmem_limit_bytes=44 * 2**20),
        name='exchange',
    )(dy, topk, slot, gates, y_back, x, h1, h3, w_gate, w_up, w_down)


def weight_grad_kernel(dx_v, dg_v, xt_v, dyd_v, actt_v, dh_v, dx_hbm, dg_hbm, dwg_hbm, dwu_hbm, dwd_hbm, stage, sem, small_sem):
    n_exp, width, _ = xt_v.shape
    ff = actt_v.shape[1]
    block = stage.shape[1]
    down = ff // block
    small = [pltpu.make_async_copy(dx_v, dx_hbm, small_sem.at[0]), pltpu.make_async_copy(dg_v, dg_hbm, small_sem.at[1])]

    def copies(u, e):
        if u < down:
            return [pltpu.make_async_copy(stage.at[u], dwd_hbm.at[e, pl.ds(u * block, block), :], sem.at[u, 0])]
        at = pl.ds((u - down) * block, block)
        return [pltpu.make_async_copy(stage.at[u, :, pl.ds(0, ff)], dwg_hbm.at[e, at, :], sem.at[u, 0]),
                pltpu.make_async_copy(stage.at[u, :, pl.ds(ff, ff)], dwu_hbm.at[e, at, :], sem.at[u, 1])]

    def one(e, carry):
        for u in range(stage.shape[0]):
            @pl.when(e > 0)
            def _():
                for copy in copies(u, e - 1):
                    copy.wait()
            if u < down:
                stage[u] = jnp.dot(actt_v[e, u * block:(u + 1) * block, :], dyd_v[e], preferred_element_type=F32)
            else:
                at = slice((u - down) * block, (u - down + 1) * block)
                stage[u] = jnp.dot(xt_v[e, at, :], dh_v[e], preferred_element_type=F32)
            for copy in copies(u, e):
                copy.start()
        return carry

    for copy in small:
        copy.start()
    lax.fori_loop(0, n_exp, one, 0)
    for u in range(stage.shape[0]):
        for copy in copies(u, n_exp - 1):
            copy.wait()
    for copy in small:
        copy.wait()


def weight_grads(dx, d_gates, xt, dyd, actt, dh):
    n_exp, width, _ = xt.shape
    ff = actt.shape[1]
    block = 256
    units = (width + ff) // block
    any_spec = pl.BlockSpec(memory_space=pl.ANY)
    vmem_spec = pl.BlockSpec(memory_space=pltpu.VMEM)
    return pl.pallas_call(
        weight_grad_kernel,
        out_shape=(
            jax.ShapeDtypeStruct(dx.shape, dx.dtype),
            jax.ShapeDtypeStruct(d_gates.shape, d_gates.dtype),
            jax.ShapeDtypeStruct((n_exp, width, ff), F32),
            jax.ShapeDtypeStruct((n_exp, width, ff), F32),
            jax.ShapeDtypeStruct((n_exp, ff, width), F32),
        ),
        in_specs=[vmem_spec] * 6,
        out_specs=(any_spec,) * 5,
        scratch_shapes=[pltpu.VMEM((units, block, width), F32), pltpu.SemaphoreType.DMA((units, 2)),
                        pltpu.SemaphoreType.DMA((2,))],
        compiler_params=pltpu.CompilerParams(vmem_limit_bytes=16 * 2**20),
        name='weight_grads',
    )(*[pltpu.with_memory_space_constraint(x, pltpu.VMEM) for x in (dx, d_gates, xt, dyd, actt, dh)])


def solution(mesh):
    ep = mesh.shape['ep']
    tok_spec = P(('dp', 'ep'), None)
    buf_spec = P(('dp', 'ep'), None, None)
    expert_spec = P('ep', None, None)

    def device_step(dy, topk_idx, slot_idx, gates, y_back, x_disp, h1_disp, h3_disp, w_gate, w_up, w_down):
        saved = exchange(
            ep, dy, topk_idx.T, slot_idx.T, gates.T, y_back, x_disp, h1_disp, h3_disp, w_gate, w_up, w_down)
        dx, d_gates, dw_gate, dw_up, dw_down = weight_grads(*saved)
        return dx, d_gates.T, dw_gate, dw_up, dw_down

    return jax.shard_map(
        device_step, mesh=mesh,
        in_specs=(tok_spec, tok_spec, tok_spec, tok_spec, buf_spec, buf_spec, buf_spec, buf_spec,
                  expert_spec, expert_spec, expert_spec),
        out_specs=(tok_spec, tok_spec, buf_spec, buf_spec, buf_spec),
        check_vma=False)
```

time: 62 us -> 55.9 us (0.902)
  Pallas kernels: 59.8 us -> 55.2 us
  local copies, waits for them, and re-layouts: 1.31 us -> 0 us
    pallas_call x2, Pallas kernels: 59.8 us -> 55.2 us  [the longest x1 43.5 us: exchange(): pl.pallas_call(functools.partial(exchange_kernel, ep, cap), out_shape=(pl...]
    unnamed x6 -> x0, local copies, waits for them, and re-layouts: 1.31 us -> none
where the time goes in v3:
time: 55.9 us
  Pallas kernels  55.2 us (99%)
  between operations  0.64 us (1%)
    pallas_call x1, Pallas kernels, exchange(): pl.pallas_call(functools.partial(exchange_kernel, ep, cap), out_shape=(pl...  43.5 us
    pallas_call x1, Pallas kernels, weight_grads(): pl.pallas_call(weight_grad_kernel, out_shape=(jax.ShapeDtypeStruct(dx.sha...  11.7 us

profile of v3, /device:TPU:81, one launch (start us, length us, event | category | flops | bytes accessed | tf_op | source)
XLA Modules:
  0.0 55.9 jit_solution(15577586511626709089)
XLA Ops:
  0.6 43.5 %exchange.1 = (bf16[128,1024]{1,0:T(8,128)(2,1)S(1)}, f32[8,128]{1,0:T(8,128)S(1)}, bf16[4,1024,512]{2,1,0:T(8,128)(2,1)S(1)}, bf16[4,512,1024]{2,1,0:T(8,128)(2...) custom-call(bf16[128,1024]{1,0:T(8,128)(2,1)} %dy_hbm.1, s32[8,128]{1,0:T(8,128)} %bitcast.4, ...), custom_call_target="tpu_custom_call" | custom-call | tf_op jit(solution)/shard_map/exchange/pallas_call | solution.py:285
  44.1 11.7 %weight_grads.1 = (bf16[128,1024]{1,0:T(8,128)(2,1)}, f32[8,128]{1,0:T(8,128)}, f32[4,1024,512]{2,1,0:T(8,128)}, f32[4,1024,512]{2,1,0:T(8,128)}, f32[4,512,1024]{2,1,0:T(8,128)}) custom-call(bf16[128,1024]{1,0:T(8,128)(2,1)S(1)} %get-tuple-element.16.dx_v, f32[8,128]{1,0:T(8,128)S(1)} %get-tuple-element.17.dg_v, ...), custom_call_target="tpu_custom_call" | custom-call | tf_op jit(solution)/shard_map/weight_grads/pallas_call | solution.py:373

commit v4 on v3

v4 whole, which is shorter than its diff:
```python
import functools
import jax
import jax.numpy as jnp
from jax import lax
from jax.experimental import pallas as pl
from jax.experimental.pallas import tpu as pltpu
from jax.sharding import PartitionSpec as P

MESH = pl.DeviceIdType.MESH
F32 = jnp.float32
BF16 = jnp.bfloat16


def dot_tn(a, b):
    return lax.dot_general(a, b, (((0,), (0,)), ((), ())), preferred_element_type=F32)


def exchange_kernel(ep, cap, dy_hbm, topk_hbm, slot_hbm, gate_hbm, yb_hbm, x_hbm, h1_hbm, h3_hbm, wg_hbm, wu_hbm, wd_hbm,
                    dx_ref, dg_ref, xt_v, dyd_v, actt_v, dh_v,
                    dyall, meta, topk_v, slot_v, square, yb_v, x_v, h1_v, h3_v, silu_v, slope_v, wgt_v, wut_v, wdt_v,
                    onehot, dxd, mine, theirs, got, fsum, fgot, own, relay, final,
                    load_sem, row_sem, meta_send, meta_recv, dy_send, dy_recv, d2d_send, d2d_recv, part_send, part_recv,
                    ring_send, ring_recv):
    chips = ep // 2
    tok, width = dyall.shape[1], dyall.shape[2]
    half = tok // 2
    n_exp, ff = wgt_v.shape[0], wgt_v.shape[1]
    top = topk_v.shape[0]
    pair = 2 * cap
    me = lax.axis_index('ep')
    chip, core = me // 2, me % 2
    right = (chip + 1) % chips
    left = (chip + chips - 1) % chips
    far = (chip + 2) % chips
    dev_r, dev_l, dev_p = right * 2 + core, left * 2 + core, chip * 2 + (1 - core)
    ahead = right * (1 - core) + left * core
    behind = left * (1 - core) + right * core
    dev_a = ahead * 2 + core
    home_of = (left * 2, right * 2, left * 2 + 1, right * 2 + 1, far * 2, far * 2 + 1, chip * 2, chip * 2 + 1)

    def remote(src, dst, send_sem, recv_sem, dev):
        return pltpu.make_async_remote_copy(src_ref=src, dst_ref=dst, send_sem=send_sem, recv_sem=recv_sem,
                                            device_id={'ep': dev}, device_id_type=MESH)

    def load(src, dst, i):
        return pltpu.make_async_copy(src, dst, load_sem.at[i])

    def by_rows(src, dst, i):
        return [pltpu.make_async_copy(src.at[:, pl.ds(pl.multiple_of(home_of[b] * cap, cap), cap), :],
                                      dst.at[:, pl.ds(b * cap, cap), :], row_sem.at[i, b]) for b in range(ep)]

    own_load = load(dy_hbm, dyall.at[me], 0)
    route_loads = [load(topk_hbm, topk_v, 1), load(slot_hbm, slot_v, 2),
                   load(gate_hbm, meta.at[me, pl.ds(top, top), :], 3)]
    h_loads = by_rows(h1_hbm, h1_v, 0) + by_rows(h3_hbm, h3_v, 1)
    wd_load, wg_load = load(wd_hbm, dyd_v, 4), load(wg_hbm, xt_v, 5)
    wu_loads = [load(wu_hbm.at[:, pl.ds(i * ff, ff), :], x_v.at[:, :, pl.ds(i * ff, ff)], 6 + i) for i in range(2)]
    yb_load = load(yb_hbm, yb_v, 8)
    x_loads = by_rows(x_hbm, x_v, 2)

    barrier = pltpu.get_barrier_semaphore()
    for d in range(1, ep):
        pl.semaphore_signal(barrier, inc=1, device_id={'ep': (me + d) % ep}, device_id_type=MESH)
    for copy in [own_load] + route_loads + h_loads + [wd_load, wg_load] + wu_loads + [yb_load]:
        copy.start()
    square[...] = jnp.zeros_like(square)
    for copy in route_loads:
        copy.wait()
    slot = slot_v[...]
    meta[me, 0:top, :] = jnp.where(slot >= 0, topk_v[...] * cap + slot, -1).astype(F32)
    own_load.wait()
    pl.semaphore_wait(barrier, ep - 1)

    def rows(ref, home, h):
        return ref.at[home, pl.ds(pl.multiple_of(h * half, half), half), :]

    def dy_copy(home, h, send_sem, recv_sem, dev):
        return remote(rows(dyall, home, h), rows(dyall, home, h), send_sem, recv_sem, dev)

    own_a = dy_copy(me, 1 - core, d2d_send.at[0], d2d_recv.at[0], dev_p)
    own_b = dy_copy(me, core, d2d_send.at[1], d2d_recv.at[1], dev_p)
    to_r = [dy_copy(chip * 2 + q, core, dy_send.at[q], dy_recv.at[q], dev_r) for q in range(2)]
    to_l = [dy_copy(chip * 2 + q, core, dy_send.at[2 + q], dy_recv.at[2 + q], dev_l) for q in range(2)]
    hop = [dy_copy(behind * 2 + q, core, dy_send.at[4 + q], dy_recv.at[4 + q], dev_a) for q in range(2)]
    left_p = [dy_copy(left * 2 + q, core, d2d_send.at[2 + q], d2d_recv.at[2 + q], dev_p) for q in range(2)]
    right_p = [dy_copy(right * 2 + q, core, d2d_send.at[4 + q], d2d_recv.at[4 + q], dev_p) for q in range(2)]
    far_p = [dy_copy(far * 2 + q, core, d2d_send.at[6 + q], d2d_recv.at[6 + q], dev_p) for q in range(2)]
    m_r, m_l, m_p, m_f, m_lp, m_rp, m_fp = metas = [
        remote(meta.at[home], meta.at[home], meta_send.at[i], meta_recv.at[i], dev) for i, (home, dev) in enumerate((
            (me, dev_r), (me, dev_l), (me, dev_p), (dev_l, dev_r), (dev_l, dev_p), (dev_r, dev_p), (far * 2 + core, dev_p)))]

    def start_first():
        to_r[0].start()
        to_l[0].start()

    own_a.start()
    pl.when(core == 0)(start_first)
    for copy in (m_r, m_l, m_p, own_b):
        copy.start()

    def factors(e, carry):
        for p in range(chips):
            span = slice(p * pair, (p + 1) * pair)
            gate_f = h1_v[e, span, :].astype(F32)
            up_f = h3_v[e, span, :].astype(F32)
            sig = jax.nn.sigmoid(gate_f)
            silu = gate_f * sig
            actt_v[e, :, span] = (silu * up_f).astype(BF16).T
            silu_v[e, span, :] = silu
            slope_v[e, span, :] = up_f * sig * (1.0 + gate_f * (1.0 - sig))
        return carry

    def build(b):
        home = home_of[b]
        table = meta[home]
        row_id = lax.broadcasted_iota(jnp.int32, (n_exp * cap, tok), 0).astype(F32) + (me * (n_exp * cap)).astype(F32)
        hit = jnp.zeros((n_exp * cap, tok), F32)
        gate = jnp.zeros((n_exp * cap, tok), F32)
        for j in range(top):
            same = row_id == table[j:j + 1, :]
            hit = jnp.where(same, 1.0, hit)
            gate = jnp.where(same, table[top + j:top + j + 1, :], gate)
        gate_row = jnp.sum(gate, axis=1, keepdims=True)
        sel = hit.astype(BF16)
        onehot[b] = sel
        for n in range(width // 256):
            cols = slice(n * 256, (n + 1) * 256)
            block = (jnp.dot(sel, dyall[home, :, cols], preferred_element_type=F32) * gate_row).astype(BF16)
            for e in range(n_exp):
                dyd_v[e, b * cap:(b + 1) * cap, cols] = block[e * cap:(e + 1) * cap]

    def experts(k, between):
        span = slice(k * pair, (k + 1) * pair)
        for e in range(n_exp):
            d_act = jnp.dot(dyd_v[e, span, :], wdt_v[e], preferred_element_type=F32).astype(BF16).astype(F32)
            dh_v[e, span, 0:ff] = (d_act * slope_v[e, span, :]).astype(BF16)
            dh_v[e, span, ff:2 * ff] = (d_act * silu_v[e, span, :]).astype(BF16)
        between()
        for e in range(n_exp):
            out = (jnp.dot(dh_v[e, span, 0:ff], wgt_v[e], preferred_element_type=F32)
                   + jnp.dot(dh_v[e, span, ff:2 * ff], wut_v[e], preferred_element_type=F32)).astype(BF16)
            for j in range(2):
                dxd[k % 2, j, e * cap:(e + 1) * cap, :] = out[j * cap:(j + 1) * cap]

    def token_sum(k, j):
        return dot_tn(onehot[2 * k + j], dxd[k % 2, j])

    def piece(h):
        return pl.ds(pl.multiple_of(h * half, half), half)

    part_a = [remote(theirs.at[q, piece(core), :], got.at[q, piece(core), :], part_send.at[q], part_recv.at[q], dev_p)
              for q in range(2)]
    part_b = [remote(theirs.at[q, piece(1 - core), :], got.at[q, piece(1 - core), :], part_send.at[2 + q],
                     part_recv.at[2 + q], dev_p) for q in range(2)]
    part_f = [remote(fsum.at[q, piece(1 - core), :], fgot.at[q], part_send.at[4 + q], part_recv.at[4 + q], dev_p)
              for q in range(2)]
    part_o = remote(own.at[1], own.at[2], part_send.at[6], part_recv.at[6], dev_p)
    one = [remote(mine.at[q, piece(1 - core), :], final.at[core, piece(1 - core), :], ring_send.at[q], ring_recv.at[core],
                  ahead * 2 + q) for q in range(2)]
    two = [remote(fsum.at[q, piece(core), :], relay.at[q], ring_send.at[2 + q], ring_recv.at[2 + q], dev_a)
           for q in range(2)]
    three = [remote(mine.at[q, piece(core), :], final.at[core, piece(core), :], ring_send.at[4 + q],
                    ring_recv.at[4 + core], ahead * 2 + q) for q in range(2)]

    def landed(direction, h, sem):
        where = final.at[direction, pl.ds(h * half, half), :]
        remote(where, where, ring_send.at[0], ring_recv.at[sem], dev_p).wait_recv()

    def next_homes():
        to_r[1].wait_recv()
        left_p[1].start()
        to_l[1].wait_recv()
        right_p[1].start()
        hop[1].start()

    def send_one(q):
        part_a[q].wait_recv()
        at = piece(1 - core)
        mine[q, at, :] = mine[q, at, :] + got[q, at, :]
        one[q].start()

    def sums(q):
        theirs[q] = token_sum(q, core)
        mine[q] = token_sum(q, 1 - core)
        part_a[q].start()
        part_b[q].start()

    for copy in h_loads:
        copy.wait()
    own_a.wait_recv()
    pl.when(core == 1)(start_first)
    to_r[1].start()
    to_l[1].start()
    lax.fori_loop(0, n_exp, factors, 0)
    m_r.wait_recv()
    m_f.start()
    m_lp.start()
    m_l.wait_recv()
    m_rp.start()

    def turn_down(e, carry):
        wdt_v[e] = dyd_v[e].T
        return carry

    def turn_gate(e, carry):
        wgt_v[e] = xt_v[e].T
        return carry

    def turn_up(e, carry):
        for i in range(2):
            wut_v[e, :, i * ff:(i + 1) * ff] = x_v[e, :, i * ff:(i + 1) * ff].T
        return carry

    wd_load.wait()
    lax.fori_loop(0, n_exp, turn_down, 0)
    wg_load.wait()
    lax.fori_loop(0, n_exp, turn_gate, 0)
    for copy in wu_loads:
        copy.wait()
    lax.fori_loop(0, n_exp, turn_up, 0)
    for copy in x_loads:
        copy.start()

    to_r[0].wait_recv()
    left_p[0].start()
    to_l[0].wait_recv()
    right_p[0].start()
    hop[0].start()
    m_lp.wait_recv()
    m_rp.wait_recv()
    left_p[0].wait_recv()
    build(0)
    right_p[0].wait_recv()
    build(1)
    experts(0, next_homes)
    sums(0)
    left_p[1].wait_recv()
    build(2)
    right_p[1].wait_recv()
    build(3)

    def far_homes():
        send_one(0)
        m_f.wait_recv()
        m_fp.start()
        for q in range(2):
            hop[q].wait_recv()
            far_p[q].start()

    experts(1, far_homes)
    sums(1)
    m_fp.wait_recv()
    for q in range(2):
        far_p[q].wait_recv()
        build(4 + q)
    experts(2, lambda: send_one(1))
    for q in range(2):
        fsum[q] = token_sum(2, q)
    for q in range(2):
        part_f[q].start()
    m_p.wait_recv()
    own_b.wait_recv()
    build(6)
    build(7)

    def send_two():
        for q in range(2):
            part_f[q].wait_recv()
            at = piece(core)
            fsum[q, at, :] = fsum[q, at, :] + fgot[q]
            two[q].start()

    send_two()
    experts(3, lambda: None)
    own[1] = token_sum(3, 1 - core)
    own[0] = token_sum(3, core)
    part_o.start()
    for q in range(2):
        part_b[q].wait_recv()
        at = piece(core)
        mine[q, at, :] = mine[q, at, :] + got[q, at, :]

    yb_load.wait()

    def gate_grad(i, carry):
        at = pl.ds(pl.multiple_of(i * 16, 16), 16)
        prod = yb_v[at].astype(F32) * dyall[me, at, :].astype(F32)[:, None, :]
        square[at, 0:top] = jnp.sum(prod, axis=-1)
        return carry
    lax.fori_loop(0, tok // 16, gate_grad, 0)
    dg_ref[...] = square[...].T[0:top, :]
    part_o.wait_recv()
    own[0] = own[0] + own[2]

    for q in range(2):
        two[q].wait_recv()
        at = piece(core)
        mine[q, at, :] = mine[q, at, :] + relay[q]
        three[q].start()
    for copy in x_loads:
        copy.wait()

    def turn(e, carry):
        for p in range(chips):
            span = slice(p * pair, (p + 1) * pair)
            xt_v[e, :, span] = x_v[e, span, :].T
        return carry
    lax.fori_loop(0, n_exp, turn, 0)
    landed(0, 1, 0)
    landed(1, 0, 1)
    landed(0, 0, 4)
    landed(1, 1, 5)
    dx_ref[...] = (own[0] + final[0] + final[1]).astype(BF16)

    for copy in metas + [own_a, own_b] + to_r + to_l + hop + left_p + right_p + far_p + part_a + part_b + part_f + [
            part_o] + one + two + three:
        copy.wait_send()


def exchange(ep, dy, topk, slot, gates, y_back, x, h1, h3, w_gate, w_up, w_down):
    tok, width = dy.shape
    n_exp, rows_e, ff = h1.shape
    cap = rows_e // ep
    top = topk.shape[0]
    any_spec = pl.BlockSpec(memory_space=pl.ANY)
    vmem_spec = pl.BlockSpec(memory_space=pltpu.VMEM)
    dma = pltpu.SemaphoreType.DMA
    return pl.pallas_call(
        functools.partial(exchange_kernel, ep, cap),
        out_shape=(
            pltpu.VMEM((tok, width), BF16),
            pltpu.VMEM((top, tok), F32),
            pltpu.VMEM((n_exp, width, rows_e), BF16),
            pltpu.VMEM((n_exp, rows_e, width), BF16),
            pltpu.VMEM((n_exp, ff, rows_e), BF16),
            pltpu.VMEM((n_exp, rows_e, 2 * ff), BF16),
        ),
        in_specs=[any_spec] * 11,
        out_specs=(vmem_spec,) * 6,
        scratch_shapes=[
            pltpu.VMEM((ep, tok, width), BF16),
            pltpu.VMEM((ep, 2 * top, tok), F32),
            pltpu.VMEM((top, tok), jnp.int32),
            pltpu.VMEM((top, tok), jnp.int32),
            pltpu.VMEM((tok, tok), F32),
            pltpu.VMEM((tok, top, width), BF16),
            pltpu.VMEM((n_exp, rows_e, width), BF16),
            pltpu.VMEM((n_exp, rows_e, ff), BF16),
            pltpu.VMEM((n_exp, rows_e, ff), BF16),
            pltpu.VMEM((n_exp, rows_e, ff), F32),
            pltpu.VMEM((n_exp, rows_e, ff), F32),
            pltpu.VMEM((n_exp, ff, width), BF16),
            pltpu.VMEM((n_exp, ff, width), BF16),
            pltpu.VMEM((n_exp, width, ff), BF16),
            pltpu.VMEM((ep, n_exp * cap, tok), BF16),
            pltpu.VMEM((2, 2, n_exp * cap, width), BF16),
            pltpu.VMEM((2, tok, width), F32),
            pltpu.VMEM((2, tok, width), F32),
            pltpu.VMEM((2, tok, width), F32),
            pltpu.VMEM((2, tok, width), F32),
            pltpu.VMEM((2, tok // 2, width), F32),
            pltpu.VMEM((3, tok, width), F32),
            pltpu.VMEM((2, tok // 2, width), F32),
            pltpu.VMEM((2, tok, width), F32),
            dma((9,)), dma((3, ep)), dma((7,)), dma((7,)), dma((6,)), dma((6,)), dma((8,)), dma((8,)),
            dma((7,)), dma((7,)), dma((6,)), dma((6,)),
        ],
        compiler_params=pltpu.CompilerParams(collective_id=0, has_side_effects=True, vmem_limit_bytes=44 * 2**20),
        name='exchange',
    )(dy, topk, slot, gates, y_back, x, h1, h3, w_gate, w_up, w_down)


def weight_grad_kernel(dx_v, dg_v, xt_v, dyd_v, actt_v, dh_v, dx_hbm, dg_hbm, dwg_hbm, dwu_hbm, dwd_hbm, stage, sem, small_sem):
    n_exp, width, _ = xt_v.shape
    ff = actt_v.shape[1]
    slots, block = stage.shape[0], stage.shape[1]
    down = ff // block
    units = [(u, e) for e in range(n_exp) for u in range((ff + width) // block)]
    small = [pltpu.make_async_copy(dx_v, dx_hbm, small_sem.at[0]), pltpu.make_async_copy(dg_v, dg_hbm, small_sem.at[1])]
    for copy in small:
        copy.start()

    def copies(i):
        (u, e), s = units[i], i % slots
        if u < down:
            return [pltpu.make_async_copy(stage.at[s], dwd_hbm.at[e, pl.ds(u * block, block), :], sem.at[s, 0])]
        at = pl.ds((u - down) * block, block)
        return [pltpu.make_async_copy(stage.at[s, :, pl.ds(0, ff)], dwg_hbm.at[e, at, :], sem.at[s, 0]),
                pltpu.make_async_copy(stage.at[s, :, pl.ds(ff, ff)], dwu_hbm.at[e, at, :], sem.at[s, 1])]

    for i, (u, e) in enumerate(units):
        if i >= slots:
            for copy in copies(i - slots):
                copy.wait()
        if u < down:
            stage[i % slots] = jnp.dot(actt_v[e, u * block:(u + 1) * block, :], dyd_v[e], preferred_element_type=F32)
        else:
            at = slice((u - down) * block, (u - down + 1) * block)
            stage[i % slots] = jnp.dot(xt_v[e, at, :], dh_v[e], preferred_element_type=F32)
        for copy in copies(i):
            copy.start()
    for i in range(len(units) - slots, len(units)):
        for copy in copies(i):
            copy.wait()
    for copy in small:
        copy.wait()


def weight_grads(dx, d_gates, xt, dyd, actt, dh):
    n_exp, width, _ = xt.shape
    ff = actt.shape[1]
    block, slots = 512, 4
    any_spec = pl.BlockSpec(memory_space=pl.ANY)
    vmem_spec = pl.BlockSpec(memory_space=pltpu.VMEM)
    return pl.pallas_call(
        weight_grad_kernel,
        out_shape=(
            jax.ShapeDtypeStruct(dx.shape, dx.dtype),
            jax.ShapeDtypeStruct(d_gates.shape, d_gates.dtype),
            jax.ShapeDtypeStruct((n_exp, width, ff), F32),
            jax.ShapeDtypeStruct((n_exp, width, ff), F32),
            jax.ShapeDtypeStruct((n_exp, ff, width), F32),
        ),
        in_specs=[vmem_spec] * 6,
        out_specs=(any_spec,) * 5,
        scratch_shapes=[pltpu.VMEM((slots, block, width), F32), pltpu.SemaphoreType.DMA((slots, 2)),
                        pltpu.SemaphoreType.DMA((2,))],
        compiler_params=pltpu.CompilerParams(vmem_limit_bytes=20 * 2**20),
        cost_estimate=pl.CostEstimate(flops=6 * n_exp * xt.shape[2] * width * ff, transcendentals=0,
                                      bytes_accessed=12 * n_exp * width * ff),
        name='weight_grads',
    )(*[pltpu.with_memory_space_constraint(x, pltpu.VMEM) for x in (dx, d_gates, xt, dyd, actt, dh)])


def solution(mesh):
    ep = mesh.shape['ep']
    tok_spec = P(('dp', 'ep'), None)
    buf_spec = P(('dp', 'ep'), None, None)
    expert_spec = P('ep', None, None)

    def device_step(dy, topk_idx, slot_idx, gates, y_back, x_disp, h1_disp, h3_disp, w_gate, w_up, w_down):
        saved = exchange(
            ep, dy, topk_idx.T, slot_idx.T, gates.T, y_back, x_disp, h1_disp, h3_disp, w_gate, w_up, w_down)
        dx, d_gates, dw_gate, dw_up, dw_down = weight_grads(*saved)
        return dx, d_gates.T, dw_gate, dw_up, dw_down

    return jax.shard_map(
        device_step, mesh=mesh,
        in_specs=(tok_spec, tok_spec, tok_spec, tok_spec, buf_spec, buf_spec, buf_spec, buf_spec,
                  expert_spec, expert_spec, expert_spec),
        out_specs=(tok_spec, tok_spec, buf_spec, buf_spec, buf_spec),
        check_vma=False)
```

time: 55.9 us -> 51.6 us (0.923)
  Pallas kernels: 55.2 us -> 50.7 us
    pallas_call x1, Pallas kernels: 11.7 us -> 9.45 us  [weight_grads(): pl.pallas_call(weight_grad_kernel, out_shape=(jax.ShapeDtypeStruct(dx.sha...]
    pallas_call x1, Pallas kernels: 43.5 us -> 41.3 us  [exchange(): pl.pallas_call(functools.partial(exchange_kernel, ep, cap), out_shape=(pl...]
where the time goes in v4:
time: 51.6 us; the launch traced here: 51.5 us
  Pallas kernels  50.7 us (98%)
  between operations  0.8 us (2%)
    pallas_call x1, Pallas kernels, exchange(): pl.pallas_call(functools.partial(exchange_kernel, ep, cap), out_shape=(pl...  41.3 us
    pallas_call x1, Pallas kernels, weight_grads(): pl.pallas_call(weight_grad_kernel, out_shape=(jax.ShapeDtypeStruct(dx.sha...  9.45 us

profile of v4, /device:TPU:81, one launch (start us, length us, event | category | flops | bytes accessed | tf_op | source)
XLA Modules:
  0.0 51.5 jit_solution(16611774048223758848)
XLA Ops:
  0.6 41.3 %exchange.1 = (bf16[128,1024]{1,0:T(8,128)(2,1)S(1)}, f32[8,128]{1,0:T(8,128)S(1)}, bf16[4,1024,512]{2,1,0:T(8,128)(2,1)S(1)}, bf16[4,512,1024]{2,1,0:T(8,128)(2...) custom-call(bf16[128,1024]{1,0:T(8,128)(2,1)} %dy_hbm.1, s32[8,128]{1,0:T(8,128)} %bitcast.4, ...), custom_call_target="tpu_custom_call" | custom-call | tf_op jit(solution)/shard_map/exchange/pallas_call | solution.py:328
  41.9 9.5 %weight_grads.1 = (bf16[128,1024]{1,0:T(8,128)(2,1)}, f32[8,128]{1,0:T(8,128)}, f32[4,1024,512]{2,1,0:T(8,128)}, f32[4,1024,512]{2,1,0:T(8,128)}, f32[4,512,1024]{2,1,0:T(8,128)}) custom-call(bf16[128,1024]{1,0:T(8,128)(2,1)S(1)} %get-tuple-element.16.dx_v, f32[8,128]{1,0:T(8,128)S(1)} %get-tuple-element.17.dg_v, ...), custom_call_target="tpu_custom_call" | custom-call | flops 6442450944 | bytes 25165824 | tf_op jit(solution)/shard_map/weight_grads/pallas_call | solution.py:415

commit v5 on v4

--- a/solution.py
+++ b/solution.py
@@ -16,7 +16,7 @@
 
 
 def exchange_kernel(ep, cap, dy_hbm, topk_hbm, slot_hbm, gate_hbm, yb_hbm, x_hbm, h1_hbm, h3_hbm, wg_hbm, wu_hbm, wd_hbm,
-                    dx_ref, dg_ref, xt_v, dyd_v, actt_v, dh_v,
+                    dx_ref, dg_ref, first_ref, xt_v, dyd_v, actt_v, dh_v,
                     dyall, meta, topk_v, slot_v, square, yb_v, x_v, h1_v, h3_v, silu_v, slope_v, wgt_v, wut_v, wdt_v,
                     onehot, dxd, mine, theirs, got, fsum, fgot, own, relay, final,
                     load_sem, row_sem, meta_send, meta_recv, dy_send, dy_recv, d2d_send, d2d_recv, part_send, part_recv,
@@ -61,7 +61,7 @@
     barrier = pltpu.get_barrier_semaphore()
     for d in range(1, ep):
         pl.semaphore_signal(barrier, inc=1, device_id={'ep': (me + d) % ep}, device_id_type=MESH)
-    for copy in [own_load] + route_loads + h_loads + [wd_load, wg_load] + wu_loads + [yb_load]:
+    for copy in [own_load] + route_loads + [wd_load, wg_load]:
         copy.start()
     square[...] = jnp.zeros_like(square)
     for copy in route_loads:
@@ -69,6 +69,8 @@
     slot = slot_v[...]
     meta[me, 0:top, :] = jnp.where(slot >= 0, topk_v[...] * cap + slot, -1).astype(F32)
     own_load.wait()
+    for copy in wu_loads:
+        copy.start()
     pl.semaphore_wait(barrier, ep - 1)
 
     def rows(ref, home, h):
@@ -97,17 +99,25 @@
     pl.when(core == 0)(start_first)
     for copy in (m_r, m_l, m_p, own_b):
         copy.start()
-
-    def factors(e, carry):
-        for p in range(chips):
-            span = slice(p * pair, (p + 1) * pair)
+    for copy in h_loads:
+        copy.start()
+
+    def factors(k):
+        span = slice(k * pair, (k + 1) * pair)
+
+        def one_expert(e, carry):
             gate_f = h1_v[e, span, :].astype(F32)
             up_f = h3_v[e, span, :].astype(F32)
             sig = jax.nn.sigmoid(gate_f)
-            silu = gate_f * sig
-            actt_v[e, :, span] = (silu * up_f).astype(BF16).T
-            silu_v[e, span, :] = silu
+            silu_v[e, span, :] = gate_f * sig
             slope_v[e, span, :] = up_f * sig * (1.0 + gate_f * (1.0 - sig))
+            return carry
+        lax.fori_loop(0, n_exp, one_expert, 0)
+
+    def activations(e, carry):
+        for k in range(chips):
+            span = slice(k * pair, (k + 1) * pair)
+            actt_v[e, :, span] = (silu_v[e, span, :] * h3_v[e, span, :].astype(F32)).astype(BF16).T
         return carry
 
     def build(b):
@@ -166,12 +176,22 @@
         where = final.at[direction, pl.ds(h * half, half), :]
         remote(where, where, ring_send.at[0], ring_recv.at[sem], dev_p).wait_recv()
 
-    def next_homes():
+    def early_r():
         to_r[1].wait_recv()
         left_p[1].start()
+
+    def early_l():
         to_l[1].wait_recv()
         right_p[1].start()
+
+    def next_homes():
+        pl.when(core == 0)(early_r)
+        pl.when(core == 1)(early_l)
         hop[1].start()
+
+    def late_homes():
+        pl.when(core == 0)(early_l)
+        pl.when(core == 1)(early_r)
 
     def send_one(q):
         part_a[q].wait_recv()
@@ -185,59 +205,67 @@
         part_a[q].start()
         part_b[q].start()
 
-    for copy in h_loads:
-        copy.wait()
+    def turn_down(e, carry):
+        wdt_v[e] = dyd_v[e].T
+        return carry
+
+    def turn_gate(e, carry):
+        wgt_v[e] = xt_v[e].T
+        return carry
+
+    def turn_up(e, carry):
+        for i in range(2):
+            wut_v[e, :, i * ff:(i + 1) * ff] = x_v[e, :, i * ff:(i + 1) * ff].T
+        return carry
+
+    wd_load.wait()
+    lax.fori_loop(0, n_exp // 2, turn_down, 0)
     own_a.wait_recv()
     pl.when(core == 1)(start_first)
-    to_r[1].start()
-    to_l[1].start()
-    lax.fori_loop(0, n_exp, factors, 0)
+    pl.when(core == 0)(to_r[1].start)
+    pl.when(core == 1)(to_l[1].start)
+    lax.fori_loop(n_exp // 2, n_exp, turn_down, 0)
     m_r.wait_recv()
     m_f.start()
     m_lp.start()
     m_l.wait_recv()
     m_rp.start()
-
-    def turn_down(e, carry):
-        wdt_v[e] = dyd_v[e].T
-        return carry
-
-    def turn_gate(e, carry):
-        wgt_v[e] = xt_v[e].T
-        return carry
-
-    def turn_up(e, carry):
-        for i in range(2):
-            wut_v[e, :, i * ff:(i + 1) * ff] = x_v[e, :, i * ff:(i + 1) * ff].T
-        return carry
-
-    wd_load.wait()
-    lax.fori_loop(0, n_exp, turn_down, 0)
     wg_load.wait()
     lax.fori_loop(0, n_exp, turn_gate, 0)
-    for copy in wu_loads:
-        copy.wait()
-    lax.fori_loop(0, n_exp, turn_up, 0)
-    for copy in x_loads:
-        copy.start()
-
     to_r[0].wait_recv()
     left_p[0].start()
     to_l[0].wait_recv()
     right_p[0].start()
     hop[0].start()
+    pl.when(core == 0)(to_l[1].start)
+    pl.when(core == 1)(to_r[1].start)
+    for copy in wu_loads:
+        copy.wait()
+    lax.fori_loop(0, n_exp, turn_up, 0)
+    for copy in x_loads + [yb_load]:
+        copy.start()
+    for copy in h_loads:
+        copy.wait()
+    factors(0)
+
     m_lp.wait_recv()
     m_rp.wait_recv()
     left_p[0].wait_recv()
+    right_p[0].wait_recv()
     build(0)
-    right_p[0].wait_recv()
     build(1)
-    experts(0, next_homes)
+    next_homes()
+    experts(0, lambda: None)
     sums(0)
+    factors(1)
+    late_homes()
+    factors(2)
+    factors(3)
     left_p[1].wait_recv()
+    right_p[1].wait_recv()
     build(2)
-    right_p[1].wait_recv()
     build(3)
+
 
     def far_homes():
         send_one(0)
@@ -252,16 +280,13 @@
     m_fp.wait_recv()
     for q in range(2):
         far_p[q].wait_recv()
-        build(4 + q)
+    build(4)
+    build(5)
     experts(2, lambda: send_one(1))
     for q in range(2):
         fsum[q] = token_sum(2, q)
     for q in range(2):
         part_f[q].start()
-    m_p.wait_recv()
-    own_b.wait_recv()
-    build(6)
-    build(7)
 
     def send_two():
         for q in range(2):
@@ -270,8 +295,11 @@
             fsum[q, at, :] = fsum[q, at, :] + fgot[q]
             two[q].start()
 
-    send_two()
-    experts(3, lambda: None)
+    m_p.wait_recv()
+    own_b.wait_recv()
+    build(6)
+    build(7)
+    experts(3, send_two)
     own[1] = token_sum(3, 1 - core)
     own[0] = token_sum(3, core)
     part_o.start()
@@ -280,6 +308,7 @@
         at = piece(core)
         mine[q, at, :] = mine[q, at, :] + got[q, at, :]
 
+    lax.fori_loop(0, n_exp, activations, 0)
     yb_load.wait()
 
     def gate_grad(i, carry):
@@ -306,6 +335,7 @@
             xt_v[e, :, span] = x_v[e, span, :].T
         return carry
     lax.fori_loop(0, n_exp, turn, 0)
+    first_ref[...] = jnp.dot(actt_v[0], dyd_v[0], preferred_element_type=F32)
     landed(0, 1, 0)
     landed(1, 0, 1)
     landed(0, 0, 4)
@@ -330,13 +360,14 @@
         out_shape=(
             pltpu.VMEM((tok, width), BF16),
             pltpu.VMEM((top, tok), F32),
+            pltpu.VMEM((ff, width), F32),
             pltpu.VMEM((n_exp, width, rows_e), BF16),
             pltpu.VMEM((n_exp, rows_e, width), BF16),
             pltpu.VMEM((n_exp, ff, rows_e), BF16),
             pltpu.VMEM((n_exp, rows_e, 2 * ff), BF16),
         ),
         in_specs=[any_spec] * 11,
-        out_specs=(vmem_spec,) * 6,
+        out_specs=(vmem_spec,) * 7,
         scratch_shapes=[
             pltpu.VMEM((ep, tok, width), BF16),
             pltpu.VMEM((ep, 2 * top, tok), F32),
@@ -370,14 +401,15 @@
     )(dy, topk, slot, gates, y_back, x, h1, h3, w_gate, w_up, w_down)
 
 
-def weight_grad_kernel(dx_v, dg_v, xt_v, dyd_v, actt_v, dh_v, dx_hbm, dg_hbm, dwg_hbm, dwu_hbm, dwd_hbm, stage, sem, small_sem):
+def weight_grad_kernel(dx_v, dg_v, first_v, xt_v, dyd_v, actt_v, dh_v, dx_hbm, dg_hbm, dwg_hbm, dwu_hbm, dwd_hbm, stage, sem, small_sem):
     n_exp, width, _ = xt_v.shape
     ff = actt_v.shape[1]
     slots, block = stage.shape[0], stage.shape[1]
     down = ff // block
-    units = [(u, e) for e in range(n_exp) for u in range((ff + width) // block)]
-    small = [pltpu.make_async_copy(dx_v, dx_hbm, small_sem.at[0]), pltpu.make_async_copy(dg_v, dg_hbm, small_sem.at[1])]
-    for copy in small:
+    units = [(u, e) for e in range(n_exp) for u in range((ff + width) // block)][ff // block:]
+    small = [pltpu.make_async_copy(dx_v, dx_hbm, small_sem.at[0]), pltpu.make_async_copy(dg_v, dg_hbm, small_sem.at[1]),
+             pltpu.make_async_copy(first_v, dwd_hbm.at[0], small_sem.at[2])]
+    for copy in small[::-1]:
         copy.start()
 
     def copies(i):
@@ -406,7 +438,7 @@
         copy.wait()
 
 
-def weight_grads(dx, d_gates, xt, dyd, actt, dh):
+def weight_grads(dx, d_gates, first, xt, dyd, actt, dh):
     n_exp, width, _ = xt.shape
     ff = actt.shape[1]
     block, slots = 512, 4
@@ -421,15 +453,15 @@
             jax.ShapeDtypeStruct((n_exp, width, ff), F32),
             jax.ShapeDtypeStruct((n_exp, ff, width), F32),
         ),
-        in_specs=[vmem_spec] * 6,
+        in_specs=[vmem_spec] * 7,
         out_specs=(any_spec,) * 5,
         scratch_shapes=[pltpu.VMEM((slots, block, width), F32), pltpu.SemaphoreType.DMA((slots, 2)),
-                        pltpu.SemaphoreType.DMA((2,))],
+                        pltpu.SemaphoreType.DMA((3,))],
         compiler_params=pltpu.CompilerParams(vmem_limit_bytes=20 * 2**20),
         cost_estimate=pl.CostEstimate(flops=6 * n_exp * xt.shape[2] * width * ff, transcendentals=0,
                                       bytes_accessed=12 * n_exp * width * ff),
         name='weight_grads',
-    )(*[pltpu.with_memory_space_constraint(x, pltpu.VMEM) for x in (dx, d_gates, xt, dyd, actt, dh)])
+    )(*[pltpu.with_memory_space_constraint(x, pltpu.VMEM) for x in (dx, d_gates, first, xt, dyd, actt, dh)])
 
 
 def solution(mesh):

time: 51.6 us -> 50.2 us (0.973)
  Pallas kernels: 50.7 us -> 49.3 us
    pallas_call x1, Pallas kernels: 41.3 us -> 40.1 us  [exchange(): pl.pallas_call(functools.partial(exchange_kernel, ep, cap), out_shape=(pl...]
where the time goes in v5:
time: 50.2 us; the launch traced here: 50.1 us
  Pallas kernels  49.3 us (98%)
  between operations  0.82 us (2%)
    pallas_call x1, Pallas kernels, exchange(): pl.pallas_call(functools.partial(exchange_kernel, ep, cap), out_shape=(pl...  40.1 us
    pallas_call x1, Pallas kernels, weight_grads(): pl.pallas_call(weight_grad_kernel, out_shape=(jax.ShapeDtypeStruct(dx.sha...  9.24 us

profile of v5, /device:TPU:81, one launch (start us, length us, event | category | flops | bytes accessed | tf_op | source)
XLA Modules:
  0.0 50.1 jit_solution(16467785993697436767)
XLA Ops:
  0.6 40.1 %exchange.1 = (bf16[128,1024]{1,0:T(8,128)(2,1)S(1)}, f32[8,128]{1,0:T(8,128)S(1)}, f32[512,1024]{1,0:T(8,128)S(1)}, bf16[4,1024,512]{2,1,0:T(8,128)(2,1)S(1)}, ...) custom-call(bf16[128,1024]{1,0:T(8,128)(2,1)} %dy_hbm.1, ...), custom_call_target="tpu_custom_call" | custom-call | tf_op jit(solution)/shard_map/exchange/pallas_call | solution.py:358
  40.7 9.2 %weight_grads.1 = (bf16[128,1024]{1,0:T(8,128)(2,1)}, f32[8,128]{1,0:T(8,128)}, f32[4,1024,512]{2,1,0:T(8,128)}, f32[4,1024,512]{2,1,0:T(8,128)}, f32[4,512,1024]{2,1,0:T(8,128)}) custom-call(bf16[128,1024]{1,0:T(8,128)(2,1)S(1)} %get-tuple-element.17.dx_v, f32[8,128]{1,0:T(8,128)S(1)} %get-tuple-element.18.dg_v, f32[512,1024]{1,0:T(8,128)S(1)} %get-tuple-element.19.first_v, ...), custom_call_target="tpu_custom_call" | custom-call | flops 6442450944 | bytes 25165824 | tf_op jit(solution)/shard_map/weight_grads/pallas_call | solution.py:447

commit v6 on v5

--- a/solution.py
+++ b/solution.py
@@ -16,7 +16,7 @@
 
 
 def exchange_kernel(ep, cap, dy_hbm, topk_hbm, slot_hbm, gate_hbm, yb_hbm, x_hbm, h1_hbm, h3_hbm, wg_hbm, wu_hbm, wd_hbm,
-                    dx_ref, dg_ref, first_ref, xt_v, dyd_v, actt_v, dh_v,
+                    acc_ref, same_ref, cross_ref, dg_ref, first_ref, xt_v, dyd_v, actt_v, dh_v,
                     dyall, meta, topk_v, slot_v, square, yb_v, x_v, h1_v, h3_v, silu_v, slope_v, wgt_v, wut_v, wdt_v,
                     onehot, dxd, mine, theirs, got, fsum, fgot, own, relay, final,
                     load_sem, row_sem, meta_send, meta_recv, dy_send, dy_recv, d2d_send, d2d_recv, part_send, part_recv,
@@ -169,8 +169,8 @@
                   ahead * 2 + q) for q in range(2)]
     two = [remote(fsum.at[q, piece(core), :], relay.at[q], ring_send.at[2 + q], ring_recv.at[2 + q], dev_a)
            for q in range(2)]
-    three = [remote(mine.at[q, piece(core), :], final.at[core, piece(core), :], ring_send.at[4 + q],
-                    ring_recv.at[4 + core], ahead * 2 + q) for q in range(2)]
+
+    first, last = slice(0, half), slice(half, tok)
 
     def landed(direction, h, sem):
         where = final.at[direction, pl.ds(h * half, half), :]
@@ -321,11 +321,6 @@
     part_o.wait_recv()
     own[0] = own[0] + own[2]
 
-    for q in range(2):
-        two[q].wait_recv()
-        at = piece(core)
-        mine[q, at, :] = mine[q, at, :] + relay[q]
-        three[q].start()
     for copy in x_loads:
         copy.wait()
 
@@ -338,12 +333,16 @@
     first_ref[...] = jnp.dot(actt_v[0], dyd_v[0], preferred_element_type=F32)
     landed(0, 1, 0)
     landed(1, 0, 1)
-    landed(0, 0, 4)
-    landed(1, 1, 5)
-    dx_ref[...] = (own[0] + final[0] + final[1]).astype(BF16)
+    acc_ref[first, :] = own[0, first, :] + final[1, first, :]
+    acc_ref[last, :] = own[0, last, :] + final[0, last, :]
+    for q in range(2):
+        two[q].wait_recv()
+        got[q, first, :] = mine[q, piece(core), :] + relay[q]
+    same_ref[...] = got[core, first, :]
+    cross_ref[...] = got[1 - core, first, :]
 
     for copy in metas + [own_a, own_b] + to_r + to_l + hop + left_p + right_p + far_p + part_a + part_b + part_f + [
-            part_o] + one + two + three:
+            part_o] + one + two:
         copy.wait_send()
 
 
@@ -358,7 +357,9 @@
     return pl.pallas_call(
         functools.partial(exchange_kernel, ep, cap),
         out_shape=(
-            pltpu.VMEM((tok, width), BF16),
+            pltpu.VMEM((tok, width), F32),
+            pltpu.VMEM((tok // 2, width), F32),
+            pltpu.VMEM((tok // 2, width), F32),
             pltpu.VMEM((top, tok), F32),
             pltpu.VMEM((ff, width), F32),
             pltpu.VMEM((n_exp, width, rows_e), BF16),
@@ -367,7 +368,7 @@
             pltpu.VMEM((n_exp, rows_e, 2 * ff), BF16),
         ),
         in_specs=[any_spec] * 11,
-        out_specs=(vmem_spec,) * 7,
+        out_specs=(vmem_spec,) * 9,
         scratch_shapes=[
             pltpu.VMEM((ep, tok, width), BF16),
             pltpu.VMEM((ep, 2 * top, tok), F32),
@@ -401,13 +402,13 @@
     )(dy, topk, slot, gates, y_back, x, h1, h3, w_gate, w_up, w_down)
 
 
-def weight_grad_kernel(dx_v, dg_v, first_v, xt_v, dyd_v, actt_v, dh_v, dx_hbm, dg_hbm, dwg_hbm, dwu_hbm, dwd_hbm, stage, sem, small_sem):
+def weight_grad_kernel(dg_v, first_v, xt_v, dyd_v, actt_v, dh_v, dg_hbm, dwg_hbm, dwu_hbm, dwd_hbm, stage, sem, small_sem):
     n_exp, width, _ = xt_v.shape
     ff = actt_v.shape[1]
     slots, block = stage.shape[0], stage.shape[1]
     down = ff // block
     units = [(u, e) for e in range(n_exp) for u in range((ff + width) // block)][ff // block:]
-    small = [pltpu.make_async_copy(dx_v, dx_hbm, small_sem.at[0]), pltpu.make_async_copy(dg_v, dg_hbm, small_sem.at[1]),
+    small = [pltpu.make_async_copy(dg_v, dg_hbm, small_sem.at[1]),
              pltpu.make_async_copy(first_v, dwd_hbm.at[0], small_sem.at[2])]
     for copy in small[::-1]:
         copy.start()
@@ -438,7 +439,7 @@
         copy.wait()
 
 
-def weight_grads(dx, d_gates, first, xt, dyd, actt, dh):
+def weight_grads(d_gates, first, xt, dyd, actt, dh):
     n_exp, width, _ = xt.shape
     ff = actt.shape[1]
     block, slots = 512, 4
@@ -447,21 +448,20 @@
     return pl.pallas_call(
         weight_grad_kernel,
         out_shape=(
-            jax.ShapeDtypeStruct(dx.shape, dx.dtype),
             jax.ShapeDtypeStruct(d_gates.shape, d_gates.dtype),
             jax.ShapeDtypeStruct((n_exp, width, ff), F32),
             jax.ShapeDtypeStruct((n_exp, width, ff), F32),
             jax.ShapeDtypeStruct((n_exp, ff, width), F32),
         ),
-        in_specs=[vmem_spec] * 7,
-        out_specs=(any_spec,) * 5,
+        in_specs=[vmem_spec] * 6,
+        out_specs=(any_spec,) * 4,
         scratch_shapes=[pltpu.VMEM((slots, block, width), F32), pltpu.SemaphoreType.DMA((slots, 2)),
                         pltpu.SemaphoreType.DMA((3,))],
         compiler_params=pltpu.CompilerParams(vmem_limit_bytes=20 * 2**20),
         cost_estimate=pl.CostEstimate(flops=6 * n_exp * xt.shape[2] * width * ff, transcendentals=0,
                                       bytes_accessed=12 * n_exp * width * ff),
         name='weight_grads',
-    )(*[pltpu.with_memory_space_constraint(x, pltpu.VMEM) for x in (dx, d_gates, first, xt, dyd, actt, dh)])
+    )(*[pltpu.with_memory_space_constraint(x, pltpu.VMEM) for x in (d_gates, first, xt, dyd, actt, dh)])
 
 
 def solution(mesh):
@@ -471,9 +471,15 @@
     expert_spec = P('ep', None, None)
 
     def device_step(dy, topk_idx, slot_idx, gates, y_back, x_disp, h1_disp, h3_disp, w_gate, w_up, w_down):
-        saved = exchange(
+        acc, same, cross, *saved = exchange(
             ep, dy, topk_idx.T, slot_idx.T, gates.T, y_back, x_disp, h1_disp, h3_disp, w_gate, w_up, w_down)
-        dx, d_gates, dw_gate, dw_up, dw_down = weight_grads(*saved)
+        ring = range(0, ep, 2)
+        same = lax.ppermute(same, 'ep', [(i, (i + 2) % ep) for i in ring] + [(i + 1, (i + 1 - 2) % ep) for i in ring])
+        cross = lax.ppermute(cross, 'ep', [(i, (i + 3) % ep) for i in ring] + [(i + 1, (i + ep - 2) % ep) for i in ring])
+        d_gates, dw_gate, dw_up, dw_down = weight_grads(*saved)
+        swap = lax.axis_index('ep') % 2 == 1
+        halves = jnp.stack([jnp.where(swap, cross, same), jnp.where(swap, same, cross)])
+        dx = (acc + halves.reshape(acc.shape)).astype(BF16)
         return dx, d_gates.T, dw_gate, dw_up, dw_down
 
     return jax.shard_map(

time: 50.2 us -> 46.4 us (0.924)
  Pallas kernels: 49.3 us -> 41.9 us
  starting transfers between devices: 0 us -> 2.84 us
  other arithmetic: 0 us -> 0.84 us
    pallas_call x1, Pallas kernels: 40.1 us -> 33.2 us  [exchange(): pl.pallas_call(functools.partial(exchange_kernel, ep, cap), out_shape=(pl...]
    ppermute x0 -> x2, starting transfers between devices: none -> 2.84 us  [the longest x1 1.81 us: device_step(): lax.ppermute(cross, 'ep', [(i, (i + 3) % ep) for i in ring] + [(i + 1, (i...]
    convert_element_type x0 -> x1, other arithmetic: none -> 0.76 us  [device_step(): dx = (acc + halves.reshape(acc.shape)).astype(BF16)]
  transfers between devices with their start and end apart: 0 -> 2, of which waited for: 0 -> 0; matrix products, arithmetic and copies ran while one was open for 0% -> 0% of each run, Pallas kernels for 0% -> 19%
where the time goes in v6:
time: 46.4 us; the launch traced here: 46.3 us
  Pallas kernels  41.9 us (90%)
  starting transfers between devices  2.84 us (6%)
  other arithmetic  0.84 us (2%)
  between operations  0.7 us (2%)
    pallas_call x1, Pallas kernels, exchange(): pl.pallas_call(functools.partial(exchange_kernel, ep, cap), out_shape=(pl...  33.2 us
    pallas_call x1, Pallas kernels, weight_grads(): pl.pallas_call(weight_grad_kernel, out_shape=(jax.ShapeDtypeStruct(d_gate...  8.75 us
    ppermute x1, starting transfers between devices, device_step(): lax.ppermute(cross, 'ep', [(i, (i + 3) % ep) for i in ring] + [(i + 1, (i...  1.81 us
    ppermute x1, starting transfers between devices, device_step(): lax.ppermute(same, 'ep', [(i, (i + 2) % ep) for i in ring] + [(i + 1, (i...  1.03 us
  transfers between devices with their start and end apart: 2, of which 0 were waited for; matrix products, arithmetic and copies ran while one was open for 0% of the time, Pallas kernels for 19%

profile of v6, /device:TPU:81, one launch (start us, length us, event | category | flops | bytes accessed | tf_op | source)
XLA Modules:
  0.0 46.3 jit_solution(15607545176530132583)
XLA Ops:
  0.6 33.2 %exchange.1 = (f32[128,1024]{1,0:T(8,128)S(1)}, f32[64,1024]{1,0:T(8,128)S(1)}, f32[64,1024]{1,0:T(8,128)S(1)}, f32[8,128]{1,0:T(8,128)S(1)}, f32[512,1024]{1,0:...) custom-call(bf16[128,1024]{1,0:T(8,128)(2,1)} %dy_hbm.1, ...), custom_call_target="tpu_custom_call" | custom-call | tf_op jit(solution)/shard_map/exchange/pallas_call | solution.py:357
  33.8 1.8 %collective-permute-start = (f32[64,1024]{1,0:T(8,128)S(1)}, f32[64,1024]{1,0:T(8,128)S(1)}, u32[]{:S(2)}, u32[]{:S(2)}) collective-permute-start(f32[64,1024]{1,0:T(8,128)S(1)} %get-tuple-element.19), channel_id=1, source_target_pairs={{0,3},{2,5},{4,7},{6,1},{1,6},{3,0},{5,2},{7,4},{8,11},{10,13},{12... | collective-permute-start | bytes 786440 | tf_op jit(solution)/shard_map/ppermute | solution.py:478
  35.6 1.0 %collective-permute-start.1 = (f32[64,1024]{1,0:T(8,128)S(1)}, f32[64,1024]{1,0:T(8,128)S(1)}, u32[]{:S(2)}, u32[]{:S(2)}) collective-permute-start(f32[64,1024]{1,0:T(8,128)S(1)} %get-tuple-element.20), channel_id=1, source_target_pairs={{0,2},{2,4},{4,6},{6,0},{1,7},{3,1},{5,3},{7,5},{8,10},{10,12},{12... | collective-permute-start | bytes 786440 | tf_op jit(solution)/shard_map/ppermute | solution.py:477
  36.6 8.7 %weight_grads.1 = (f32[8,128]{1,0:T(8,128)}, f32[4,1024,512]{2,1,0:T(8,128)}, f32[4,1024,512]{2,1,0:T(8,128)}, f32[4,512,1024]{2,1,0:T(8,128)}) custom-call(f32[8,128]{1,0:T(8,128)S(1)} %get-tuple-element.21.dg_v, f32[512,1024]{1,0:T(8,128)S(1)} %get-tuple-element.22.first_v, bf16[4,1024,512]{2,1,0:T(8,128)(2,1)S(1)} %get-tuple-element.23.xt_v, ...), custom_call_target="tpu_custom_call" | custom-call | flops 6442450944 | bytes 25165824 | tf_op jit(solution)/shard_map/weight_grads/pallas_call | solution.py:448
  45.4 0.0 collective-permute-done
  45.4 0.0 collective-permute-done.1
  45.5 0.8 %fusion = bf16[128,1024]{1,0:T(8,128)(2,1)} fusion(f32[128,1024]{1,0:T(8,128)S(1)} %get-tuple-element.18, f32[2,64,1024]{2,1,0:T(8,128)S(1)} %pad_maximum_fusion), kind=kLoop, calls=%fused_computation.2 | loop fusion | flops 262144 | bytes 1310720 | tf_op jit(solution)/shard_map/convert_element_type | solution.py:482
  (2 shorter events, 0.1 us)
Async XLA Ops:
  33.8 11.6 %collective-permute-start = (f32[64,1024]{1,0:T(8,128)S(1)}, f32[64,1024]{1,0:T(8,128)S(1)}, u32[]{:S(2)}, u32[]{:S(2)}) collective-permute-start(f32[64,1024]{1,0:T(8,128)S(1)} %get-tuple-element.19), channel_id=1, source_target_pairs={{0,3},{2,5},{4,7},{6,1},{1,6},{3,0},{5,2},{7,4},{8,11},{10,13},{12... | collective-permute-start | bytes 786440 | tf_op jit(solution)/shard_map/ppermute | solution.py:478
  35.6 9.8 %collective-permute-start.1 = (f32[64,1024]{1,0:T(8,128)S(1)}, f32[64,1024]{1,0:T(8,128)S(1)}, u32[]{:S(2)}, u32[]{:S(2)}) collective-permute-start(f32[64,1024]{1,0:T(8,128)S(1)} %get-tuple-element.20), channel_id=1, source_target_pairs={{0,2},{2,4},{4,6},{6,0},{1,7},{3,1},{5,3},{7,5},{8,10},{10,12},{12... | collective-permute-start | bytes 786440 | tf_op jit(solution)/shard_map/ppermute | solution.py:477
